TPU v7x, 32 devices: a whole 2x2x4 slice. The times are simulated.
32 devices in a mesh: dp: 8 (over z, y), head: 4 (over x, core).
Axes of the slice: x: 2, y: 2, z: 4, core: 2. Of those that a mesh axis runs over, the one named last changes fastest.
Arguments:
- tokens: bfloat16 [3, 8192, 768], P(None, ('dp', 'head')), may hold values from -6 to 6
- cotangent: bfloat16 [3, 8192, 768], P(None, ('dp', 'head')), may hold values from -6 to 6
- bucket_ids: int32 [3, 16], P(None, 'dp'), may hold values from 0 to 2, as said below
- seq_lengths: int32 [3, 16, 8], P(None, 'dp'), may hold values from 0 to 256, as said below
- query_weight: bfloat16 [768, 768], P('dp', 'head'), may hold values from -0.3125 to 0.3125
- query_bias: bfloat16 [12, 64], P('head', 'dp'), may hold values from -3 to 3
- key_weight: bfloat16 [768, 768], P('dp', 'head'), may hold values from -0.21875 to 0.21875
- value_weight: bfloat16 [768, 768], P('dp', 'head'), may hold values from -0.21875 to 0.21875
- value_bias: bfloat16 [12, 64], P('head', 'dp'), may hold values from -3 to 3
- output_weight: bfloat16 [768, 768], P(('dp', 'head')), may hold values from -0.875 to 0.875
- output_bias: bfloat16 [768], P(('dp', 'head')), may hold values from -3 to 3
- first_gain: bfloat16 [768], P(('dp', 'head')), may hold values from 0.25 to 1.75
- first_shift: bfloat16 [768], P(('dp', 'head')), may hold values from -3 to 3
- inner_weight: bfloat16 [768, 3072], P(('dp', 'head')), may hold values from -0.21875 to 0.21875
- inner_bias: bfloat16 [3072], P(('dp', 'head')), may hold values from -3 to 3
- outer_weight: bfloat16 [3072, 768], P(('dp', 'head')), may hold values from -0.109375 to 0.109375
- outer_bias: bfloat16 [768], P(('dp', 'head')), may hold values from -3 to 3
- second_gain: bfloat16 [768], P(('dp', 'head')), may hold values from 0.25 to 1.75
- second_shift: bfloat16 [768], P(('dp', 'head')), may hold values from -3 to 3
Outputs:
- layer_out: bfloat16 [3, 8192, 768], P(None, ('dp', 'head'))
- input_grad: bfloat16 [3, 8192, 768], P(None, ('dp', 'head'))
- grad_query_weight: float32 [768, 768], P('dp', 'head')
- grad_query_bias: float32 [12, 64], P('head', 'dp')
- grad_key_weight: float32 [768, 768], P('dp', 'head')
- grad_value_weight: float32 [768, 768], P('dp', 'head')
- grad_value_bias: float32 [12, 64], P('head', 'dp')
- grad_output_weight: float32 [768, 768], P(('dp', 'head'))
- grad_output_bias: float32 [768], P(('dp', 'head'))
- grad_first_gain: float32 [768], P(('dp', 'head'))
- grad_first_shift: float32 [768], P(('dp', 'head'))
- grad_inner_weight: float32 [768, 3072], P(('dp', 'head'))
- grad_inner_bias: float32 [3072], P(('dp', 'head'))
- grad_outer_weight: float32 [3072, 768], P(('dp', 'head'))
- grad_outer_bias: float32 [768], P(('dp', 'head'))
- grad_second_gain: float32 [768], P(('dp', 'head'))
- grad_second_shift: float32 [768], P(('dp', 'head'))
Inputs may be any that keep to these rules, and one draw needn't show every extreme that they name: `bucket_ids`: every micro-batch has some block of bucket 2 and some block of bucket 0; a block of bucket b holds 8 / 2^b sequences of 64 * 2^b rows each. `seq_lengths`: in a block of bucket b the first 8 / 2^b entries are lengths from 1 to 64 * 2^b and the others are 0; in every micro-batch some block holds a sequence of length 256.
All inputs are finite; a program needn't handle non-finite values.
Results may differ from a plain program's by a relative error of at most 0.017.
Values may be sent and summed in bfloat16 or wider, within the bound.
A program may use at most 128 MiB of HBM per device.

v0:
```python
import jax
import jax.numpy as jnp
from jax import lax
from jax.sharding import PartitionSpec as P

HD = 64
SHORT = 64
SLOTS = 8
MICRO = 3
BLOCK = 512


NEG_FILL = -1e30
SQRT_HALF = 0.7071067811865476
INV_SQRT_TAU = 0.3989422804014327


def gelu_erf(values):
    return 0.5 * values * (1.0 + lax.erf(values * SQRT_HALF))


def gelu_slope(values):
    return 0.5 * (1.0 + lax.erf(values * SQRT_HALF)) + values * INV_SQRT_TAU * jnp.exp(
        -0.5 * values * values
    )


def norm_forward(values, gain_row, shift_row):
    centered = values - jnp.mean(values, axis=-1, keepdims=True)
    inverse_scale = lax.rsqrt(jnp.mean(centered * centered, axis=-1, keepdims=True) + 1e-12)
    normed = centered * inverse_scale
    return (normed * gain_row + shift_row, normed, inverse_scale)


def norm_backward(grad_out, normed, inverse_scale, gain_row):
    scaled = grad_out * gain_row
    grad_in = inverse_scale * (
        scaled
        - jnp.mean(scaled, axis=-1, keepdims=True)
        - normed * jnp.mean(scaled * normed, axis=-1, keepdims=True)
    )
    return (grad_in, jnp.sum(grad_out * normed, axis=0), jnp.sum(grad_out, axis=0))


def block_mask(bucket, seq_lens):
    seq_width = SHORT * jnp.where(bucket == 0, 1, jnp.where(bucket == 1, 2, 4)).astype(jnp.int32)
    positions = jnp.arange(BLOCK, dtype=jnp.int32)
    member_seq = positions // seq_width
    within_seq = positions % seq_width
    lookup_table = (member_seq[:, None] == jnp.arange(SLOTS, dtype=jnp.int32)[None, :]).astype(
        jnp.int32
    )
    key_limit = jnp.sum(lookup_table * seq_lens[None, :], axis=1)
    return (member_seq[:, None] == member_seq[None, :]) & (within_seq < key_limit)[None, :]


def masked_scores(query_blk, key_blk, allowed):
    scale = query_blk.shape[-1] ** (-0.5)
    scores = (
        jnp.einsum("qhd,khd->hqk", query_blk, key_blk, preferred_element_type=jnp.float32) * scale
    )
    return jnp.where(allowed[None], scores, NEG_FILL)


def attend_forward(packed):
    query_blk, key_blk, value_blk, bucket, seq_lens = packed
    scores = masked_scores(query_blk, key_blk, block_mask(bucket, seq_lens))
    row_top = jnp.max(scores, axis=-1, keepdims=True)
    powered = jnp.exp(scores - row_top)
    totals = jnp.sum(powered, axis=-1, keepdims=True)
    probs_low = (powered / totals).astype(jnp.bfloat16)
    attended = jnp.einsum("hqk,khd->qhd", probs_low, value_blk, preferred_element_type=jnp.float32)
    return (attended.astype(jnp.bfloat16), (row_top + jnp.log(totals))[..., 0])


def attend_backward(packed):
    query_blk, key_blk, value_blk, bucket, seq_lens, log_total, grad_blk = packed
    scale = query_blk.shape[-1] ** (-0.5)
    scores = masked_scores(query_blk, key_blk, block_mask(bucket, seq_lens))
    softmax_out = jnp.exp(scores - log_total[..., None])
    grad_probs = jnp.einsum("qhd,khd->hqk", grad_blk, value_blk, preferred_element_type=jnp.float32)
    row_inner = jnp.sum(grad_probs * softmax_out, axis=-1, keepdims=True)
    grad_scores = (softmax_out * (grad_probs - row_inner)).astype(jnp.bfloat16)
    grad_query = (
        jnp.einsum("hqk,khd->qhd", grad_scores, key_blk, preferred_element_type=jnp.float32) * scale
    ).astype(jnp.bfloat16)
    grad_key = (
        jnp.einsum("hqk,qhd->khd", grad_scores, query_blk, preferred_element_type=jnp.float32)
        * scale
    ).astype(jnp.bfloat16)
    grad_value = jnp.einsum(
        "hqk,qhd->khd",
        softmax_out.astype(jnp.bfloat16),
        grad_blk,
        preferred_element_type=jnp.float32,
    ).astype(jnp.bfloat16)
    return (grad_query, grad_key, grad_value)


def micro_batch(token_rows, grad_rows, buckets, seq_lens, attn_now, dense_now):
    query_full, key_full, value_full, query_bias_full, value_bias_full = attn_now
    (
        proj_full,
        proj_bias,
        gain_first,
        shift_first,
        inner_full,
        inner_bias_full,
        outer_full,
        outer_bias_full,
        gain_second,
        shift_second,
    ) = dense_now
    gain_first = gain_first.astype(jnp.float32)
    gain_second = gain_second.astype(jnp.float32)
    group_rows = lax.all_gather(token_rows, "head", axis=0, tiled=True)
    query_rows = (
        jnp.dot(group_rows, query_full, preferred_element_type=jnp.float32)
        + query_bias_full.reshape(-1).astype(jnp.float32)
    ).astype(jnp.bfloat16)
    key_rows = jnp.dot(group_rows, key_full, preferred_element_type=jnp.float32).astype(
        jnp.bfloat16
    )
    value_rows = (
        jnp.dot(group_rows, value_full, preferred_element_type=jnp.float32)
        + value_bias_full.reshape(-1).astype(jnp.float32)
    ).astype(jnp.bfloat16)
    block_shape = (buckets.shape[0], BLOCK, query_full.shape[1] // HD, HD)
    query_blocks = query_rows.reshape(block_shape)
    key_blocks = key_rows.reshape(block_shape)
    value_blocks = value_rows.reshape(block_shape)
    attended, log_total = lax.map(
        attend_forward, (query_blocks, key_blocks, value_blocks, buckets, seq_lens)
    )
    head_rows = attended.reshape(query_rows.shape)
    mixed_rows = lax.all_to_all(head_rows, "head", split_axis=0, concat_axis=1, tiled=True)
    branch_out = jnp.dot(
        mixed_rows, proj_full, preferred_element_type=jnp.float32
    ) + proj_bias.astype(jnp.float32)
    first_out, first_normed, first_scale = norm_forward(
        token_rows.astype(jnp.float32) + branch_out, gain_first, shift_first.astype(jnp.float32)
    )
    first_low = first_out.astype(jnp.bfloat16)
    hidden_pre = jnp.dot(
        first_low, inner_full, preferred_element_type=jnp.float32
    ) + inner_bias_full.astype(jnp.float32)
    active_low = gelu_erf(hidden_pre).astype(jnp.bfloat16)
    second_in = (
        first_out
        + jnp.dot(active_low, outer_full, preferred_element_type=jnp.float32)
        + outer_bias_full.astype(jnp.float32)
    )
    layer_out, second_normed, second_scale = norm_forward(
        second_in, gain_second, shift_second.astype(jnp.float32)
    )
    grad_out = grad_rows.astype(jnp.float32)
    grad_second, grad_gain_two, grad_shift_two = norm_backward(
        grad_out, second_normed, second_scale, gain_second
    )
    grad_outer_low = grad_second.astype(jnp.bfloat16)
    grad_outer_weight = jnp.einsum(
        "tf,td->fd", active_low, grad_outer_low, preferred_element_type=jnp.float32
    )
    grad_outer_bias = jnp.sum(grad_outer_low.astype(jnp.float32), axis=0)
    grad_active = jnp.einsum(
        "td,fd->tf", grad_outer_low, outer_full, preferred_element_type=jnp.float32
    )
    grad_hidden_low = (grad_active * gelu_slope(hidden_pre)).astype(jnp.bfloat16)
    grad_inner_weight = jnp.einsum(
        "td,tf->df", first_low, grad_hidden_low, preferred_element_type=jnp.float32
    )
    grad_inner_bias = jnp.sum(grad_hidden_low.astype(jnp.float32), axis=0)
    grad_first = grad_second + jnp.einsum(
        "tf,df->td", grad_hidden_low, inner_full, preferred_element_type=jnp.float32
    )
    grad_branch, grad_gain_one, grad_shift_one = norm_backward(
        grad_first, first_normed, first_scale, gain_first
    )
    grad_branch_low = grad_branch.astype(jnp.bfloat16)
    grad_proj_weight = jnp.einsum(
        "tc,td->cd", mixed_rows, grad_branch_low, preferred_element_type=jnp.float32
    )
    grad_proj_bias = jnp.sum(grad_branch_low.astype(jnp.float32), axis=0)
    grad_mixed = jnp.einsum(
        "td,cd->tc", grad_branch_low, proj_full, preferred_element_type=jnp.float32
    ).astype(jnp.bfloat16)
    grad_heads = lax.all_to_all(grad_mixed, "head", split_axis=1, concat_axis=0, tiled=True)
    grad_query, grad_key, grad_value = lax.map(
        attend_backward,
        (
            query_blocks,
            key_blocks,
            value_blocks,
            buckets,
            seq_lens,
            log_total,
            grad_heads.reshape(block_shape),
        ),
    )
    grad_query = grad_query.reshape(query_rows.shape)
    grad_key = grad_key.reshape(query_rows.shape)
    grad_value = grad_value.reshape(query_rows.shape)
    grad_query_weight = jnp.einsum(
        "td,tc->dc", group_rows, grad_query, preferred_element_type=jnp.float32
    )
    grad_key_weight = jnp.einsum(
        "td,tc->dc", group_rows, grad_key, preferred_element_type=jnp.float32
    )
    grad_value_weight = jnp.einsum(
        "td,tc->dc", group_rows, grad_value, preferred_element_type=jnp.float32
    )
    grad_query_bias = jnp.sum(grad_query.astype(jnp.float32), axis=0).reshape(query_bias_full.shape)
    grad_value_bias = jnp.sum(grad_value.astype(jnp.float32), axis=0).reshape(value_bias_full.shape)
    grad_group = (
        jnp.einsum("tc,dc->td", grad_query, query_full, preferred_element_type=jnp.float32)
        + jnp.einsum("tc,dc->td", grad_key, key_full, preferred_element_type=jnp.float32)
        + jnp.einsum("tc,dc->td", grad_value, value_full, preferred_element_type=jnp.float32)
    )
    grad_token = lax.psum_scatter(
        grad_group.astype(jnp.bfloat16), "head", scatter_dimension=0, tiled=True
    ).astype(jnp.float32)
    input_grad = (grad_branch + grad_token).astype(jnp.bfloat16)
    attn_grads = (
        grad_query_weight,
        grad_key_weight,
        grad_value_weight,
        grad_query_bias,
        grad_value_bias,
    )
    dense_grads = (
        grad_proj_weight,
        grad_proj_bias,
        grad_gain_one,
        grad_shift_one,
        grad_inner_weight,
        grad_inner_bias,
        grad_outer_weight,
        grad_outer_bias,
        grad_gain_two,
        grad_shift_two,
    )
    return (layer_out.astype(jnp.bfloat16), input_grad, attn_grads, dense_grads)


def body(
    tokens,
    cotangent,
    bucket_ids,
    seq_lengths,
    query_weight,
    query_bias,
    key_weight,
    value_weight,
    value_bias,
    output_weight,
    output_bias,
    first_gain,
    first_shift,
    inner_weight,
    inner_bias,
    outer_weight,
    outer_bias,
    second_gain,
    second_shift,
):
    layer_outs = []
    input_grads = []
    attn_total = None
    dense_total = None
    for micro_step in range(MICRO):
        attn_now = (
            lax.all_gather(query_weight, "dp", axis=0, tiled=True),
            lax.all_gather(key_weight, "dp", axis=0, tiled=True),
            lax.all_gather(value_weight, "dp", axis=0, tiled=True),
            lax.all_gather(query_bias, "dp", axis=1, tiled=True),
            lax.all_gather(value_bias, "dp", axis=1, tiled=True),
        )
        dense_now = (
            lax.all_gather(output_weight, ("dp", "head"), axis=0, tiled=True),
            lax.all_gather(output_bias, ("dp", "head"), axis=0, tiled=True),
            lax.all_gather(first_gain, ("dp", "head"), axis=0, tiled=True),
            lax.all_gather(first_shift, ("dp", "head"), axis=0, tiled=True),
            lax.all_gather(inner_weight, ("dp", "head"), axis=0, tiled=True),
            lax.all_gather(inner_bias, ("dp", "head"), axis=0, tiled=True),
            lax.all_gather(outer_weight, ("dp", "head"), axis=0, tiled=True),
            lax.all_gather(outer_bias, ("dp", "head"), axis=0, tiled=True),
            lax.all_gather(second_gain, ("dp", "head"), axis=0, tiled=True),
            lax.all_gather(second_shift, ("dp", "head"), axis=0, tiled=True),
        )
        layer_out, input_grad, attn_grads, dense_grads = micro_batch(
            tokens[micro_step],
            cotangent[micro_step],
            bucket_ids[micro_step],
            seq_lengths[micro_step],
            attn_now,
            dense_now,
        )
        layer_outs.append(layer_out)
        input_grads.append(input_grad)
        if attn_total is None:
            attn_total = tuple(attn_grads)
            dense_total = tuple(dense_grads)
        else:
            attn_total = tuple(jax.tree.map(jnp.add, attn_total, tuple(attn_grads)))
            dense_total = tuple(jax.tree.map(jnp.add, dense_total, tuple(dense_grads)))
    attn_total = (
        lax.psum_scatter(attn_total[0], "dp", scatter_dimension=0, tiled=True),
        lax.psum_scatter(attn_total[1], "dp", scatter_dimension=0, tiled=True),
        lax.psum_scatter(attn_total[2], "dp", scatter_dimension=0, tiled=True),
        lax.psum_scatter(attn_total[3], "dp", scatter_dimension=1, tiled=True),
        lax.psum_scatter(attn_total[4], "dp", scatter_dimension=1, tiled=True),
    )
    dense_total = (
        lax.psum_scatter(dense_total[0], ("dp", "head"), scatter_dimension=0, tiled=True),
        lax.psum_scatter(dense_total[1], ("dp", "head"), scatter_dimension=0, tiled=True),
        lax.psum_scatter(dense_total[2], ("dp", "head"), scatter_dimension=0, tiled=True),
        lax.psum_scatter(dense_total[3], ("dp", "head"), scatter_dimension=0, tiled=True),
        lax.psum_scatter(dense_total[4], ("dp", "head"), scatter_dimension=0, tiled=True),
        lax.psum_scatter(dense_total[5], ("dp", "head"), scatter_dimension=0, tiled=True),
        lax.psum_scatter(dense_total[6], ("dp", "head"), scatter_dimension=0, tiled=True),
        lax.psum_scatter(dense_total[7], ("dp", "head"), scatter_dimension=0, tiled=True),
        lax.psum_scatter(dense_total[8], ("dp", "head"), scatter_dimension=0, tiled=True),
        lax.psum_scatter(dense_total[9], ("dp", "head"), scatter_dimension=0, tiled=True),
    )
    return (
        jnp.stack(layer_outs),
        jnp.stack(input_grads),
        attn_total[0],
        attn_total[3],
        attn_total[1],
        attn_total[2],
        attn_total[4],
        dense_total[0],
        dense_total[1],
        dense_total[2],
        dense_total[3],
        dense_total[4],
        dense_total[5],
        dense_total[6],
        dense_total[7],
        dense_total[8],
        dense_total[9],
    )


def solution(mesh):
    placed = (
        P(None, ("dp", "head"), None),
        P(None, ("dp", "head"), None),
        P(None, "dp"),
        P(None, "dp", None),
        P("dp", "head"),
        P("head", "dp"),
        P("dp", "head"),
        P("dp", "head"),
        P("head", "dp"),
        P(("dp", "head"), None),
        P(("dp", "head")),
        P(("dp", "head")),
        P(("dp", "head")),
        P(("dp", "head"), None),
        P(("dp", "head")),
        P(("dp", "head"), None),
        P(("dp", "head")),
        P(("dp", "head")),
        P(("dp", "head")),
    )
    return jax.shard_map(
        body,
        mesh=mesh,
        in_specs=placed,
        out_specs=(
            P(None, ("dp", "head"), None),
            P(None, ("dp", "head"), None),
            P("dp", "head"),
            P("head", "dp"),
            P("dp", "head"),
            P("dp", "head"),
            P("head", "dp"),
            P(("dp", "head"), None),
            P(("dp", "head")),
            P(("dp", "head")),
            P(("dp", "head")),
            P(("dp", "head"), None),
            P(("dp", "head")),
            P(("dp", "head"), None),
            P(("dp", "head")),
            P(("dp", "head")),
            P(("dp", "head")),
        ),
        check_vma=False,
    )
```

profile of v0, /device:TPU:0, one launch (start us, length us, event | category | flops | bytes accessed | tf_op | source)
XLA Modules:
  0.0 1085.1 jit_solution(15186154365319889830)
XLA Ops:
  14.7 42.8 %all-reduce.18 = (bf16[768]{0:T(1024)(128)(2,1)S(1)}, bf16[768]{0:T(1024)(128)(2,1)S(1)}, bf16[768]{0:T(1024)(128)(2,1)S(1)}, bf16[768]{0:T(1024)(128)(2,1)S(1)}...) all-reduce(bf16[768]{0:T(1024)(128)(2,1)S(1)} %dynamic-update-slice, ...), channel_id=1, replica_groups=mesh['dp'=8,'head'=4] {'dp','head'}, use_global_device_ids=true, to_apply=%add | all-reduce | flops 7680 | bytes 30720
  59.3 31.0 %all_gather.37 = bf16[768,192]{1,0:T(8,128)(2,1)S(1)} all-gather(bf16[96,192]{1,0:T(8,128)(2,1)S(1)} %copy-done.102), channel_id=1, replica_groups=mesh['dp'=8,'head'=4] {'dp'}, dimensions={0}, use_global_device_ids=true | all-gather | bytes 331776 | tf_op jit(solution)/shard_map/all_gather | solution.py:274
  90.3 20.5 %all-gather.3 = bf16[8,8,3]{1,2,0:T(4,128)(2,1)S(1)} all-gather(bf16[1,8,3]{1,2,0:T(4,128)(2,1)S(1)} %bitcast.739), channel_id=1, replica_groups=mesh['dp'=8,'head'=4] {'dp'}, dimensions={0}, use_global_device_ids=true | all-gather | bytes 432 | tf_op jit(solution)/shard_map/all_gather | solution.py:276
  112.2 31.4 %all_gather.39 = bf16[768,192]{1,0:T(8,128)(2,1)S(1)} all-gather(bf16[96,192]{1,0:T(8,128)(2,1)S(1)} %copy-done.103), channel_id=1, replica_groups=mesh['dp'=8,'head'=4] {'dp'}, dimensions={0}, use_global_device_ids=true | all-gather | bytes 331776 | tf_op jit(solution)/shard_map/all_gather | solution.py:272
  143.6 16.3 %all-gather.4 = bf16[8,8,3]{1,2,0:T(4,128)(2,1)S(1)} all-gather(bf16[1,8,3]{1,2,0:T(4,128)(2,1)S(1)} %bitcast.740), channel_id=1, replica_groups=mesh['dp'=8,'head'=4] {'dp'}, dimensions={0}, use_global_device_ids=true | all-gather | bytes 432 | tf_op jit(solution)/shard_map/all_gather | solution.py:275
  160.7 31.7 %all_gather.41 = bf16[768,192]{1,0:T(8,128)(2,1)S(1)} all-gather(bf16[96,192]{1,0:T(8,128)(2,1)S(1)} %copy-done.104), channel_id=1, replica_groups=mesh['dp'=8,'head'=4] {'dp'}, dimensions={0}, use_global_device_ids=true | all-gather | bytes 331776 | tf_op jit(solution)/shard_map/all_gather | solution.py:273
  201.8 12.8 %while.92 = (s32[]{:T(128)}, bf16[2,512,3,64]{1,3,2,0:T(8,128)(2,1)S(1)}, f32[2,3,512]{2,1,0:T(4,128)S(1)}, bf16[2,512,3,64]{1,3,2,0:T(8,128)(2,1)S(1)}, s32[2]{...) while((s32[]{:T(128)}, ...), condition=%wide.region_22.23_spmd, body=%wide.region_18.22_spmd.sunk | while | flops 211404800 | bytes 11345269 | solution.py:132
  216.6 4.6 all-to-all-start.2
  230.9 12.8 %while.91 = (s32[]{:T(128)}, bf16[2,512,3,64]{1,3,2,0:T(8,128)(2,1)S(1)}, f32[2,3,512]{2,1,0:T(4,128)S(1)}, bf16[2,512,3,64]{1,3,2,0:T(8,128)(2,1)}, s32[2]{0:T(...) while((s32[]{:T(128)}, ...), condition=%wide.region_13.14_spmd, body=%wide.region_9.13_spmd.sunk | while | flops 211404800 | bytes 12918161 | solution.py:132
  260.0 11.5 %while.90 = (s32[]{:T(128)}, bf16[2,512,3,64]{1,3,2,0:T(8,128)(2,1)S(1)}, f32[2,3,512]{2,1,0:T(4,128)S(1)}, bf16[2,512,3,64]{1,3,2,0:T(8,128)(2,1)}, s32[2]{0:T(...) while((s32[]{:T(128)}, ...), condition=%wide.region_4.5_spmd, body=%wide.region_0.4_spmd.sunk | while | flops 211404800 | bytes 12918161 | solution.py:132
  277.0 4.3 all-to-all-start.1
  284.9 3.9 all-to-all-done.1
  288.8 4.1 all-to-all-start
  297.0 3.4 all-to-all-done
  303.1 5.8 convolution_add_fusion
  308.9 5.0 fusion.395
  340.7 3.6 convert_reduce_fusion.11
  347.8 3.5 all-to-all-start.5
  360.6 4.1 all-to-all-start.4
  371.3 18.2 %while.95 = (s32[]{:T(128)}, bf16[2,512,3,64]{1,3,2,0:T(8,128)(2,1)}, bf16[2,512,3,64]{1,3,2,0:T(8,128)(2,1)}, bf16[2,512,3,64]{1,3,2,0:T(8,128)(2,1)}, bf16[2,5...) while((s32[]{:T(128)}, ...), condition=%wide.region_52.53_spmd, body=%wide.region_49.52_spmd.sunk | while | flops 511428608 | bytes 37143188 | solution.py:188
  396.6 4.2 all-to-all-start.3
  404.9 17.8 %while.94 = (s32[]{:T(128)}, bf16[2,512,3,64]{1,3,2,0:T(8,128)(2,1)}, bf16[2,512,3,64]{1,3,2,0:T(8,128)(2,1)}, bf16[2,512,3,64]{1,3,2,0:T(8,128)(2,1)}, bf16[2,5...) while((s32[]{:T(128)}, ...), condition=%wide.region_43.44_spmd, body=%wide.region_40.43_spmd.sunk | while | flops 511428608 | bytes 37143120 | solution.py:188
  434.7 15.0 %while.93 = (s32[]{:T(128)}, bf16[2,512,3,64]{1,3,2,0:T(8,128)(2,1)S(1)}, bf16[2,512,3,64]{1,3,2,0:T(8,128)(2,1)}, bf16[2,512,3,64]{1,3,2,0:T(8,128)(2,1)}, bf16...) while((s32[]{:T(128)}, ...), condition=%wide.region_34.35_spmd, body=%wide.region_31.34_spmd.sunk | while | flops 511428608 | bytes 32424444 | solution.py:188
  483.2 6.8 add_add_fusion.1
  494.9 7.9 add_add_fusion
  511.6 39.6 %all-reduce.16 = (f32[768]{0:T(1024)}, f32[768]{0:T(1024)}, f32[768]{0:T(1024)}, f32[3072]{0:T(1024)}, f32[768]{0:T(1024)}, /*index=5*/f32[768]{0:T(1024)}, f32[768]{0:T(1024)S(1)}) all-reduce(f32[768]{0:T(1024)} %add_add_fusion.9, f32[768]{0:T(1024)} %add_add_fusion.8, ...), channel_id=14, replica_groups=mesh['dp'=8,'head'=4] {'dp','head'}, use_global_device_ids=true, to_apply=%region_69.70.clone | all-reduce | flops 7680 | bytes 61440
  563.6 20.3 %all-reduce.17 = (f32[3,64]{1,0:T(4,128)S(1)}, f32[3,64]{1,0:T(4,128)S(1)}) all-reduce(f32[3,64]{1,0:T(4,128)S(1)} %add_add_fusion.11, f32[3,64]{1,0:T(4,128)S(1)} %add_add_fusion.10), channel_id=9, replica_groups=mesh['dp'=8,'head'=4] {'dp'}, use_global_device_ids=true, to_apply=%region_58.59.clone | all-reduce | flops 384 | bytes 3072
  589.7 34.9 %reduce-scatter.32.cloned.1.call-done = f32[96,192]{1,0:T(8,128)} async-done(((f32[768,192]{1,0:T(8,128)}), f32[96,192]{1,0:T(8,128)}) %reduce-scatter.32.cloned.1.call-update) | async-done | bytes 73744
  624.5 66.0 %reduce-scatter.34.cloned.1.call-done = f32[96,192]{1,0:T(8,128)} async-done(((f32[768,192]{1,0:T(8,128)}), f32[96,192]{1,0:T(8,128)}) %reduce-scatter.34.cloned.1.call-update) | async-done | bytes 73744
  690.6 104.5 %reduce-scatter.24.cloned.1.call-done = f32[24,768]{1,0:T(8,128)} async-done(((f32[768,768]{1,0:T(8,128)}), f32[24,768]{1,0:T(8,128)}) %reduce-scatter.24.cloned.1.call-update) | async-done | bytes 73744 | tf_op jit(solution)/shard_map/reduce_scatter | solution.py:314
  795.1 141.6 %reduce-scatter.26.cloned.1.call-done = f32[24,3072]{1,0:T(8,128)} async-done(((f32[768,3072]{1,0:T(8,128)}), f32[24,3072]{1,0:T(8,128)}) %reduce-scatter.26.cloned.1.call-update) | async-done | bytes 294928 | tf_op jit(solution)/shard_map/reduce_scatter | solution.py:318
  936.7 141.5 %reduce-scatter.28.cloned.1.call-done = f32[96,768]{1,0:T(8,128)} async-done(((f32[3072,768]{1,0:T(8,128)}), f32[96,768]{1,0:T(8,128)}) %reduce-scatter.28.cloned.1.call-update) | async-done | bytes 294928 | tf_op jit(solution)/shard_map/reduce_scatter | solution.py:320
  (743 shorter events, 267.4 us)
Async XLA Ops:
  7.3 83.0 %copy-start.135 = (bf16[3,8]{1,0:T(4,128)(2,1)S(1)}, bf16[3,8]{1,0:T(4,128)(2,1)}, u32[]{:S(2)}) copy-start(bf16[3,8]{1,0:T(4,128)(2,1)} %param.39) | copy-start | bytes 148
  7.3 103.7 %copy-start.122 = (s32[3,2]{0,1:T(2,128)S(1)}, s32[3,2]{0,1:T(2,128)}, u32[]{:S(2)}) copy-start(s32[3,2]{0,1:T(2,128)} %param.33) | copy-start | bytes 76
  7.3 104.4 %copy-start.134 = (s32[3,2,8]{2,1,0:T(2,128)S(1)}, s32[3,2,8]{2,1,0:T(2,128)}, u32[]{:S(2)}) copy-start(s32[3,2,8]{2,1,0:T(2,128)} %param.34) | copy-start | bytes 580
  7.3 104.9 %copy-start.103 = (bf16[96,192]{1,0:T(8,128)(2,1)S(1)}, bf16[96,192]{1,0:T(8,128)(2,1)}, u32[]{:S(2)}) copy-start(bf16[96,192]{1,0:T(8,128)(2,1)} %param.35) | copy-start | bytes 110596
  7.3 136.3 %copy-start.136 = (bf16[3,8]{1,0:T(4,128)(2,1)S(1)}, bf16[3,8]{1,0:T(4,128)(2,1)}, u32[]{:S(2)}) copy-start(bf16[3,8]{1,0:T(4,128)(2,1)} %param.36) | copy-start | bytes 148
  7.3 153.3 %copy-start.104 = (bf16[96,192]{1,0:T(8,128)(2,1)S(1)}, bf16[96,192]{1,0:T(8,128)(2,1)}, u32[]{:S(2)}) copy-start(bf16[96,192]{1,0:T(8,128)(2,1)} %param.37) | copy-start | bytes 110596
  7.3 185.7 %all-gather.22.cloned.1.call-start = ((), (), s32[]{:S(2)}) async-start(), calls=%async_computation.26 | async-start | bytes 1966080 | tf_op jit(solution)/shard_map/all_gather | solution.py:116
  9.7 211.5 %all-gather.20.cloned.1.call-start = ((), (), s32[]{:S(2)}) async-start(), calls=%async_computation.25 | async-start | bytes 1966080 | tf_op jit(solution)/shard_map/all_gather | solution.py:116
  10.5 234.5 %all-gather.18.cloned.1.call-start = ((), (), s32[]{:S(2)}) async-start(), calls=%async_computation.24 | async-start | bytes 1966080 | tf_op jit(solution)/shard_map/all_gather | solution.py:116
  11.2 270.1 %all-gather.12.cloned.1.call-start = ((), (), s32[]{:S(2)}) async-start(), calls=%async_computation.15 | async-start | bytes 1216512 | tf_op jit(solution)/shard_map/all_gather | solution.py:279
  11.8 291.3 %all-gather.14.cloned.1.call-start = ((), (), s32[]{:S(2)}) async-start(), calls=%async_computation.16 | async-start | bytes 4866048 | tf_op jit(solution)/shard_map/all_gather | solution.py:283
  12.4 296.5 %all-gather.16.cloned.1.call-start = ((), (), s32[]{:S(2)}) async-start(), calls=%async_computation.17 | async-start | bytes 4866048 | tf_op jit(solution)/shard_map/all_gather | solution.py:285
  192.4 127.6 %copy-start.95 = (f32[768]{0:T(1024)}, f32[768]{0:T(1024)S(1)}, u32[]{:S(2)}) copy-start(f32[768]{0:T(1024)S(1)} %convert_element_type.432) | copy-start | bytes 9220
  192.4 152.0 %copy-start.93 = (f32[768]{0:T(1024)}, f32[768]{0:T(1024)S(1)}, u32[]{:S(2)}) copy-start(f32[768]{0:T(1024)S(1)} %convert_element_type.431) | copy-start | bytes 9220
  216.6 60.4 %all-to-all-start.2 = ((bf16[4,256,192]{1,2,0:T(8,128)(2,1)}), bf16[4,256,192]{1,2,0:T(8,128)(2,1)}, u32[]{:S(2)}, u32[]{:S(2)}) async-start(bf16[4,256,192]{1,2,0:T(8,128)(2,1)} %copy.274), calls=%async_computation.2 | async-start | bytes 786432 | tf_op jit(solution)/shard_map/all_to_all | solution.py:136
  277.0 11.8 %all-to-all-start.1 = ((bf16[4,256,192]{1,2,0:T(8,128)(2,1)}), bf16[4,256,192]{1,2,0:T(8,128)(2,1)}, u32[]{:S(2)}, u32[]{:S(2)}) async-start(bf16[4,256,192]{1,2,0:T(8,128)(2,1)} %copy.269), calls=%async_computation.1 | async-start | bytes 786432 | tf_op jit(solution)/shard_map/all_to_all | solution.py:136
  288.8 11.6 %all-to-all-start = ((bf16[4,256,192]{1,2,0:T(8,128)(2,1)}), bf16[4,256,192]{1,2,0:T(8,128)(2,1)}, u32[]{:S(2)}, u32[]{:S(2)}) async-start(bf16[4,256,192]{1,2,0:T(8,128)(2,1)} %copy.264), calls=%async_computation | async-start | bytes 786432 | tf_op jit(solution)/shard_map/all_to_all | solution.py:136
  347.8 12.8 %all-to-all-start.5 = ((bf16[256,4,192]{0,2,1:T(8,128)(2,1)}), bf16[256,4,192]{0,2,1:T(8,128)(2,1)S(1)}, u32[]{:S(2)}, u32[]{:S(2)}) async-start(bf16[256,4,192]{0,2,1:T(8,128)(2,1)} %bitcast.727), calls=%async_computation.7 | async-start | bytes 786432 | tf_op jit(solution)/shard_map/all_to_all | solution.py:187
  360.6 36.0 %all-to-all-start.4 = ((bf16[256,4,192]{0,2,1:T(8,128)(2,1)}), bf16[256,4,192]{0,2,1:T(8,128)(2,1)}, u32[]{:S(2)}, u32[]{:S(2)}) async-start(bf16[256,4,192]{0,2,1:T(8,128)(2,1)} %bitcast.92), calls=%async_computation.5 | async-start | bytes 786432 | tf_op jit(solution)/shard_map/all_to_all | solution.py:187
  364.7 220.6 %reduce-scatter.22.cloned.1.call-start = ((), (), s32[]{:S(2)}) async-start(), calls=%async_computation.20 | async-start | bytes 1966080 | tf_op jit(solution)/shard_map/reduce_scatter | solution.py:219
  396.6 29.7 %all-to-all-start.3 = ((bf16[256,4,192]{0,2,1:T(8,128)(2,1)}), bf16[256,4,192]{0,2,1:T(8,128)(2,1)}, u32[]{:S(2)}, u32[]{:S(2)}) async-start(bf16[256,4,192]{0,2,1:T(8,128)(2,1)} %bitcast.88), calls=%async_computation.3 | async-start | bytes 786432 | tf_op jit(solution)/shard_map/all_to_all | solution.py:187
  400.9 185.5 %reduce-scatter.20.cloned.1.call-start = ((), (), s32[]{:S(2)}) async-start(), calls=%async_computation.19 | async-start | bytes 1966080 | tf_op jit(solution)/shard_map/reduce_scatter | solution.py:219
  433.0 154.4 %reduce-scatter.18.cloned.1.call-start = ((), (), s32[]{:S(2)}) async-start(), calls=%async_computation.18 | async-start | bytes 1966080 | tf_op jit(solution)/shard_map/reduce_scatter | solution.py:219
  455.5 134.2 %reduce-scatter.30.cloned.1.call-start = ((), (), s32[]{:S(2)}) async-start(), calls=%async_computation.27 | async-start | bytes 884736
  461.9 162.6 %reduce-scatter.32.cloned.1.call-start = ((), (), s32[]{:S(2)}) async-start(), calls=%async_computation.28 | async-start | bytes 884736
  467.7 222.9 %reduce-scatter.34.cloned.1.call-start = ((), (), s32[]{:S(2)}) async-start(), calls=%async_computation.29 | async-start | bytes 884736
  471.8 323.3 %reduce-scatter.24.cloned.1.call-start = ((), (), s32[]{:S(2)}) async-start(), calls=%async_computation.21 | async-start | bytes 2433024 | tf_op jit(solution)/shard_map/reduce_scatter | solution.py:314
  478.0 458.7 %reduce-scatter.26.cloned.1.call-start = ((), (), s32[]{:S(2)}) async-start(), calls=%async_computation.22 | async-start | bytes 9732096 | tf_op jit(solution)/shard_map/reduce_scatter | solution.py:318
  490.1 588.0 %reduce-scatter.28.cloned.1.call-start = ((), (), s32[]{:S(2)}) async-start(), calls=%async_computation.23 | async-start | bytes 9732096 | tf_op jit(solution)/shard_map/reduce_scatter | solution.py:320
  505.0 57.9 %copy-start.42 = (bf16[2,512,3,64]{1,3,2,0:T(8,128)(2,1)S(1)}, bf16[2,512,3,64]{1,3,2,0:T(8,128)(2,1)}, u32[]{:S(2)}) copy-start(bf16[2,512,3,64]{1,3,2,0:T(8,128)(2,1)} %copy-done.41) | copy-start | bytes 1179652
  505.0 58.2 %copy-start.52 = (bf16[2,512,3,64]{1,3,2,0:T(8,128)(2,1)S(1)}, bf16[2,512,3,64]{1,3,2,0:T(8,128)(2,1)}, u32[]{:S(2)}) copy-start(bf16[2,512,3,64]{1,3,2,0:T(8,128)(2,1)} %get-tuple-element.2109) | copy-start | bytes 1179652
  505.0 58.3 %copy-start.46 = (bf16[2,512,3,64]{1,3,2,0:T(8,128)(2,1)S(1)}, bf16[2,512,3,64]{1,3,2,0:T(8,128)(2,1)}, u32[]{:S(2)}) copy-start(bf16[2,512,3,64]{1,3,2,0:T(8,128)(2,1)} %get-tuple-element.746) | copy-start | bytes 1179652
  (162 other events, 698.3 us)
Sparse Core Ops, SparseCore 0:
  10.3 22.9 all-gather.21
  34.8 19.6 all-gather.19
  56.6 19.6 all-gather.17
  79.0 54.5 all-gather.11
  136.4 63.8 all-gather.13
  203.0 62.1 all-gather.15
  396.7 27.5 reduce-scatter.21
  433.1 27.6 reduce-scatter.19
  463.3 27.9 reduce-scatter.17
  495.1 63.2 reduce-scatter.29
  562.3 62.2 reduce-scatter.31
  628.3 62.2 reduce-scatter.33
  696.4 98.6 reduce-scatter.23
  801.4 135.2 reduce-scatter.25
  943.0 135.1 reduce-scatter.27
where the time goes:
time: 1100 us; the launch traced here: 1090 us
  waiting for transfers between devices  499 us (45%)
  blocking collectives  234 us (21%)
  matrix products  143 us (13%)
  local copies, waits for them, and re-layouts  107 us (10%)
  other arithmetic  43 us (4%)
  starting transfers between devices  25.6 us (2%)
  loops' own time  17.4 us (2%)
  between operations  17.2 us (2%)
    reduce_scatter x1, waiting for transfers between devices, body(): lax.psum_scatter(dense_total[4], ('dp', 'head'), scatter_dimension=0, til...  142 us
    reduce_scatter x1, waiting for transfers between devices, body(): lax.psum_scatter(dense_total[6], ('dp', 'head'), scatter_dimension=0, til...  141 us
    reduce_scatter x1, waiting for transfers between devices, body(): lax.psum_scatter(dense_total[0], ('dp', 'head'), scatter_dimension=0, til...  105 us
    unnamed x18, waiting for transfers between devices  104 us
    unnamed x3, blocking collectives  103 us
    all_gather x1, blocking collectives, body(): lax.all_gather(key_weight, 'dp', axis=0, tiled=True)  31.7 us
    all_gather x1, blocking collectives, body(): lax.all_gather(query_weight, 'dp', axis=0, tiled=True)  31.4 us
    all_gather x1, blocking collectives, body(): lax.all_gather(value_weight, 'dp', axis=0, tiled=True)  31 us
  transfers between devices with their start and end apart: 21, of which 7 were waited for; matrix products, arithmetic and copies ran while one was open for 22% of the time, Pallas kernels for 0%

commit v1 on v0

v1 whole, which is shorter than its diff:
```python
import jax
import jax.numpy as jnp
from jax import lax
from jax.sharding import PartitionSpec as P

HD = 64
SHORT = 64
SLOTS = 8
BLOCK = 512
LONGEST = 256

NEG_FILL = -1e30
SQRT_HALF = 0.7071067811865476
INV_SQRT_TAU = 0.3989422804014327
F32 = jnp.float32
BF16 = jnp.bfloat16


def norm_forward(values):
    centered = values - jnp.mean(values, axis=-1, keepdims=True)
    inverse_scale = lax.rsqrt(jnp.mean(centered * centered, axis=-1, keepdims=True) + 1e-12)
    return centered * inverse_scale, inverse_scale


def norm_backward(grad_out, normed, inverse_scale, gain_row):
    scaled = grad_out * gain_row
    return inverse_scale * (
        scaled
        - jnp.mean(scaled, axis=-1, keepdims=True)
        - normed * jnp.mean(scaled * normed, axis=-1, keepdims=True)
    )


def local_mask(bucket_ids, seq_lengths, rows):
    start = lax.axis_index("head") * rows
    block = start // BLOCK
    bucket = lax.dynamic_index_in_dim(bucket_ids, block, axis=1, keepdims=True)
    lens = lax.dynamic_index_in_dim(seq_lengths, block, axis=1, keepdims=False)
    width = SHORT * jnp.where(bucket == 0, 1, jnp.where(bucket == 1, 2, 4)).astype(jnp.int32)
    place = start % BLOCK + jnp.arange(rows, dtype=jnp.int32)[None, :]
    member = place // width
    within = place % width
    hit = (member[:, :, None] == jnp.arange(SLOTS, dtype=jnp.int32)[None, None, :]).astype(jnp.int32)
    limit = jnp.sum(hit * lens[:, None, :], axis=2)
    return (member[:, :, None] == member[:, None, :]) & (within < limit)[:, None, :]


def mm(a, b):
    return jnp.dot(a, b, preferred_element_type=F32)


def mm_nt(a, b):
    return lax.dot_general(a, b, (((1,), (1,)), ((), ())), preferred_element_type=F32)


def mm_tn(a, b):
    return lax.dot_general(a, b, (((0,), (0,)), ((), ())), preferred_element_type=F32)


def layer(x, dy, mask, p):
    micro, rows, width = x.shape
    heads = width // HD
    n = micro * rows
    x = x.reshape(n, width)
    dy = dy.reshape(n, width).astype(F32)
    (wq, qb, wk, wv, vb, wo, ob, g1, s1, wi, ib, wu, ub, g2, s2) = p
    f = lambda v: v.reshape(1, -1).astype(F32)
    shape = (micro, rows, heads, HD)
    q = (mm(x, wq) + f(qb)).astype(BF16).reshape(shape)
    k = mm(x, wk).astype(BF16).reshape(shape)
    v = (mm(x, wv) + f(vb)).astype(BF16).reshape(shape)
    scores = jnp.einsum("mqhd,mkhd->mhqk", q, k, preferred_element_type=F32) * HD**-0.5
    scores = jnp.where(mask[:, None], scores, NEG_FILL)
    top = jnp.max(scores, axis=-1, keepdims=True)
    powered = jnp.exp(scores - top)
    probs = powered / jnp.sum(powered, axis=-1, keepdims=True)
    att = jnp.einsum("mhqk,mkhd->mqhd", probs.astype(BF16), v, preferred_element_type=F32)
    att = att.astype(BF16).reshape(n, width)
    z1, q1 = norm_forward(x.astype(F32) + mm(att, wo) + f(ob))
    first = z1 * f(g1) + f(s1)
    first_low = first.astype(BF16)
    pre = mm(first_low, wi) + f(ib)
    cdf = 0.5 * (1.0 + lax.erf(pre * SQRT_HALF))
    active = (pre * cdf).astype(BF16)
    z2, q2 = norm_forward(first + mm(active, wu) + f(ub))
    out = (z2 * f(g2) + f(s2)).astype(BF16)
    g_second = norm_backward(dy, z2, q2, f(g2))
    g_outer = g_second.astype(BF16)
    slope = cdf + pre * INV_SQRT_TAU * jnp.exp(-0.5 * pre * pre)
    g_hidden = (mm_nt(g_outer, wu) * slope).astype(BF16)
    g_first = g_second + mm_nt(g_hidden, wi)
    g_branch = norm_backward(g_first, z1, q1, f(g1))
    g_branch_low = g_branch.astype(BF16)
    g_att = mm_nt(g_branch_low, wo).astype(BF16).reshape(shape)
    dprobs = jnp.einsum("mqhd,mkhd->mhqk", g_att, v, preferred_element_type=F32)
    inner = jnp.sum(dprobs * probs, axis=-1, keepdims=True)
    ds = (probs * (dprobs - inner)).astype(BF16)
    scale = HD**-0.5
    gq = (jnp.einsum("mhqk,mkhd->mqhd", ds, k, preferred_element_type=F32) * scale).astype(BF16)
    gk = (jnp.einsum("mhqk,mqhd->mkhd", ds, q, preferred_element_type=F32) * scale).astype(BF16)
    gv = jnp.einsum("mhqk,mqhd->mkhd", probs.astype(BF16), g_att, preferred_element_type=F32).astype(BF16)
    gq, gk, gv = (g.reshape(n, width) for g in (gq, gk, gv))
    g_in = (g_branch + mm_nt(gq, wq) + mm_nt(gk, wk) + mm_nt(gv, wv)).astype(BF16)
    rs = lambda g: jnp.sum(g.astype(F32), axis=0)
    big = (mm_tn(x, gq), mm_tn(x, gk), mm_tn(x, gv), mm_tn(att, g_branch_low), mm_tn(first_low, g_hidden), mm_tn(active, g_outer))
    small = (rs(gq), rs(gv), rs(g_branch_low), rs(g_first * z1), rs(g_first), rs(g_hidden), rs(g_outer), rs(dy * z2), rs(dy))
    return out.reshape(micro, rows, width), g_in.reshape(micro, rows, width), big, small


def body(tokens, cotangent, bucket_ids, seq_lengths, wq, qb, wk, wv, vb, wo, ob, g1, s1, wi, ib, wu, ub, g2, s2):
    both = ("dp", "head")
    rows = tokens.shape[1]
    assert rows % LONGEST == 0
    ag = lambda a, ax, dim: lax.all_gather(a, ax, axis=dim, tiled=True)
    n_head = lax.axis_size("head")
    wqkv = ag(jnp.stack([wq, wk, wv]), "dp", 1)
    wqkv = ag(wqkv, "head", 2)
    ob_, g1_, s1_, ub_, g2_, s2_, ib_ = (ag(a, both, 0) for a in (ob, g1, s1, ub, g2, s2, ib))
    qb_, vb_ = (ag(ag(a, "dp", 1), "head", 0) for a in (qb, vb))
    p = (wqkv[0], qb_, wqkv[1], wqkv[2], vb_, ag(wo, both, 0), ob_, g1_, s1_, ag(wi, both, 0), ib_, ag(wu, both, 0), ub_, g2_, s2_)
    mask = local_mask(bucket_ids, seq_lengths, rows)
    out, g_in, big, small = layer(tokens, cotangent, mask, p)
    sc = lambda a, ax, dim: lax.psum_scatter(a, ax, scatter_dimension=dim, tiled=True)
    gqkv = jnp.stack([b.astype(BF16) for b in big[:3]])
    gqkv = sc(sc(gqkv, "head", 2), "dp", 1).astype(F32)
    go, gi, gu = (sc(b.astype(BF16), both, 0).astype(F32) for b in big[3:])
    hb = lambda a: sc(sc(a.reshape(-1, HD), "head", 0), "dp", 1)
    s = small
    return (out, g_in, gqkv[0], hb(s[0]), gqkv[1], gqkv[2], hb(s[1]), go, sc(s[2], both, 0), sc(s[3], both, 0), sc(s[4], both, 0), gi, sc(s[5], both, 0), gu, sc(s[6], both, 0), sc(s[7], both, 0), sc(s[8], both, 0))


def solution(mesh):
    rows = P(None, ("dp", "head"), None)
    dense = P(("dp", "head"), None)
    flat = P(("dp", "head"))
    tile = P("dp", "head")
    bias = P("head", "dp")
    params = (tile, bias, tile, tile, bias, dense, flat, flat, flat, dense, flat, dense, flat, flat, flat)
    return jax.shard_map(
        body,
        mesh=mesh,
        in_specs=(rows, rows, P(None, "dp"), P(None, "dp", None)) + params,
        out_specs=(rows, rows) + params,
        check_vma=False,
    )
```

time: 1100 us -> 793 us (0.72)
  waiting for transfers between devices: 499 us -> 383 us
  local copies, waits for them, and re-layouts: 107 us -> 47.9 us
  blocking collectives: 234 us -> 195 us
  matrix products: 143 us -> 115 us
  starting transfers between devices: 25.6 us -> 0.36 us
  loops' own time: 17.4 us -> 0 us
  other arithmetic: 43 us -> 30.6 us
    reduce_scatter x6 -> x4, waiting for transfers between devices: 388 us -> 245 us  [body(): lax.psum_scatter(a, ax, scatter_dimension=dim, tiled=True)]
    all_gather x6 -> x4, waiting for transfers between devices: 0.07 us -> 70.7 us  [body(): ag = lambda a, ax, dim: lax.all_gather(a, ax, axis=dim, tiled=True)]
    all_gather x5, blocking collectives: 131 us -> 83.9 us  [body(): ag = lambda a, ax, dim: lax.all_gather(a, ax, axis=dim, tiled=True)]
    unnamed x18 -> x10, waiting for transfers between devices: 104 us -> 66.8 us
    dot_general x96 -> x23, matrix products: 143 us -> 107 us  [the longest x6 33.2 us: mm(): return jnp.dot(a, b, preferred_element_type=F32)]
    all_to_all x6 -> x0, starting transfers between devices: 24.8 us -> none  [the longest x3 13 us: micro_batch(): lax.all_to_all(head_rows, 'head', split_axis=0, concat_axis=1, tiled=True)]
    while x108 -> x0, local copies, waits for them, and re-layouts: 23.5 us -> none  [the longest x12 10.1 us: micro_batch(): lax.map(attend_backward, (query_blocks, key_blocks, value_blocks, buckets...]
    another operation x6 -> x0, loops' own time: 17.4 us -> none  [the longest x3 9.27 us: micro_batch(): lax.map(attend_backward, (query_blocks, key_blocks, value_blocks, buckets...]
  transfers between devices with their start and end apart: 21 -> 9, of which waited for: 7 -> 7; matrix products, arithmetic and copies ran while one was open for 22% -> 13% of each run, Pallas kernels for 0% -> 0%
where the time goes in v1:
time: 793 us; the launch traced here: 788 us
  waiting for transfers between devices  383 us (48%)
  blocking collectives  195 us (25%)
  matrix products  115 us (15%)
  local copies, waits for them, and re-layouts  47.9 us (6%)
  other arithmetic  30.6 us (4%)
  between operations  16.2 us (2%)
    reduce_scatter x4, waiting for transfers between devices, body(): lax.psum_scatter(a, ax, scatter_dimension=dim, tiled=True)  245 us
    unnamed x4, blocking collectives  111 us
    all_gather x5, blocking collectives, body(): ag = lambda a, ax, dim: lax.all_gather(a, ax, axis=dim, tiled=True)  83.9 us
    all_gather x4, waiting for transfers between devices, body(): ag = lambda a, ax, dim: lax.all_gather(a, ax, axis=dim, tiled=True)  70.7 us
    unnamed x10, waiting for transfers between devices  66.8 us
    dot_general x6, matrix products, mm(): return jnp.dot(a, b, preferred_element_type=F32)  33.2 us
    dot_general x6, matrix products, mm_tn(): lax.dot_general(a, b, (((0,), (0,)), ((), ())), preferred_element_type=F32)  25.5 us
    unnamed x149, local copies, waits for them, and re-layouts  24.9 us
  transfers between devices with their start and end apart: 9, of which 7 were waited for; matrix products, arithmetic and copies ran while one was open for 13% of the time, Pallas kernels for 0%

profile of v1, /device:TPU:0, one launch (start us, length us, event | category | flops | bytes accessed | tf_op | source)
XLA Modules:
  0.0 788.4 jit_solution(9514672448216281075)
XLA Ops:
  8.3 38.7 %all_gather.48 = bf16[3,768,192]{2,0,1:T(4,128)(2,1)S(1)} all-gather(bf16[3,96,192]{2,0,1:T(4,128)(2,1)S(1)} %copy.145), channel_id=1, replica_groups=mesh['dp'=8,'head'=4] {'dp'}, dimensions={1}, use_global_device_ids=true | all-gather | bytes 995328 | tf_op jit(solution)/shard_map/all_gather | solution.py:114
  51.3 18.6 %all-gather.2 = bf16[8,8,3]{1,2,0:T(4,128)(2,1)S(1)} all-gather(bf16[1,8,3]{1,2,0:T(4,128)(2,1)S(1)} %bitcast.178), channel_id=1, replica_groups=mesh['dp'=8,'head'=4] {'dp'}, dimensions={0}, use_global_device_ids=true | all-gather | bytes 432 | tf_op jit(solution)/shard_map/all_gather | solution.py:114
  70.0 5.2 all-gather.3
  75.3 16.3 %all-gather = bf16[8,8,3]{1,2,0:T(4,128)(2,1)S(1)} all-gather(bf16[1,8,3]{1,2,0:T(4,128)(2,1)S(1)} %bitcast.179), channel_id=1, replica_groups=mesh['dp'=8,'head'=4] {'dp'}, dimensions={0}, use_global_device_ids=true | all-gather | bytes 432 | tf_op jit(solution)/shard_map/all_gather | solution.py:114
  91.7 5.1 all-gather.1
  98.5 39.0 %all-reduce.21 = (bf16[768]{0:T(1024)(128)(2,1)S(1)}, bf16[768]{0:T(1024)(128)(2,1)S(1)}, bf16[768]{0:T(1024)(128)(2,1)S(1)}, bf16[3072]{0:T(1024)(128)(2,1)S(1)...) all-reduce(bf16[768]{0:T(1024)(128)(2,1)S(1)} %dynamic-update-slice, ...), channel_id=1, replica_groups=mesh['dp'=8,'head'=4] {'dp','head'}, use_global_device_ids=true, to_apply=%add | all-reduce | flops 7680 | bytes 30720
  148.8 4.3 fusion.36
  156.9 3.8 fusion.28
  160.6 3.7 reshape.407
  164.4 8.3 %fusion.80 = (f32[3,12,256]{2,1,0:T(8,128)S(1)}, f32[3,12,256,256]{2,3,1,0:T(8,128)}) fusion(pred[3,256,256]{1,2,0:T(8,128)(4,1)S(1)} %compare_and_fusion, bf16[3,256,12,64]{1,0,3,2:T(4,128)(2,1)} %reshape.409, bf16[3,256,12,64]{1,0,3,2:T(4,128)(2,1)S(1)} %reshape.408), kind=kOutput, calls=%fused_computation.141 | convolution fusion | flops 311427328 | bytes 12029952 | tf_op jit(solution)/shard_map/sub | solution.py:75
  172.6 5.1 fusion.33
  184.9 16.7 %all-gather.13.cloned.1.call-done = bf16[768,3072]{1,0:T(8,128)(2,1)} async-done(((bf16[24,3072]{1,0:T(8,128)(2,1)}), bf16[768,3072]{1,0:T(8,128)(2,1)}) %all-gather.13.cloned.1.call-update) | async-done | bytes 4718608 | tf_op jit(solution)/shard_map/all_gather | solution.py:114
  201.6 10.8 %multiply_convert_fusion.1 = (bf16[768,3072]{1,0:T(8,128)(2,1)}, f32[768,3072]{1,0:T(8,128)}) fusion(f32[3072]{0:T(1024)} %convert_element_type.213, bf16[768,3072]{1,0:T(8,128)(2,1)} %all-gather.13.cloned.1.call-done, f32[768,768]{1,0:T(8,128)S(1)} %get-tuple-element.160, f32[768]{0:T(1024)} %convert_element_type.211, f32[768]{0:T(1024)S(1)} %copy-done.23, ...), kind=kOutput, calls=%fused_computation.10 | convolution fusion | flops 3640983552 | bytes 21258240 | tf_op jit(solution)/shard_map/dot_general | solution.py:49
  212.3 54.0 %all-gather.15.cloned.1.call-done = bf16[3072,768]{1,0:T(8,128)(2,1)} async-done(((bf16[96,768]{1,0:T(8,128)(2,1)}), bf16[3072,768]{1,0:T(8,128)(2,1)}) %all-gather.15.cloned.1.call-update) | async-done | bytes 4718608 | tf_op jit(solution)/shard_map/all_gather | solution.py:114
  266.3 7.5 fusion.90
  278.5 10.7 %convert_reduce_fusion = (f32[3072]{0:T(1024)}, bf16[768,3072]{1,0:T(8,128)(2,1)S(1)}) fusion(f32[768,3072]{1,0:T(8,128)} %get-tuple-element.162, f32[3072]{0:T(1024)S(1)} %copy-done.29, bf16[3072,768]{1,0:T(8,128)(2,1)S(1)} %copy-done.38, f32[768,768]{1,0:T(8,128)S(1)} %get-tuple-element.146), kind=kOutput, calls=%fused_computation.7 | convolution fusion | flops 3655136256 | bytes 21258240 | tf_op jit(solution)/shard_map/dot_general | solution.py:53
  289.2 5.0 multiply_reduce_fusion.1
  305.0 6.4 convert_reduce_fusion.4
  311.5 7.1 multiply_reduce_fusion
  318.6 11.2 %multiply_convert_fusion = bf16[3,12,256,256]{2,3,1,0:T(8,128)(2,1)} fusion(f32[3,12,256,256]{2,3,1,0:T(8,128)} %get-tuple-element.167, f32[3,12,256]{2,1,0:T(8,128)S(1)} %get-tuple-element.166, f32[3,12,256,256]{2,3,1,0:T(8,128)} %get-tuple-element.158, f32[3,12,256]{2,1,0:T(8,128)S(1)} %copy-done.20), kind=kLoop, calls=%fused_computation.8 | loop fusion | flops 9437184 | bytes 23666688 | tf_op jit(solution)/shard_map/convert_element_type | solution.py:97
  329.8 4.1 convert_reduce_fusion.5
  347.0 4.3 convolution_convert_fusion.2
  351.4 9.3 %convolution_convert_fusion.1 = bf16[768,3072]{1,0:T(8,128)(2,1)} fusion(bf16[768,3072]{1,0:T(8,128)(2,1)} %copy-done.51, f32[768,768]{1,0:T(8,128)S(1)} %copy-done.5, f32[768]{0:T(1024)} %convert_element_type.211, f32[768]{0:T(1024)S(1)} %copy-done.24, f32[768]{0:T(1024)} %add_rsqrt_fusion.1, f32[768]{0:T(1024)S(1)} %broadcast_multiply_fusion.5), kind=kOutput, calls=%fused_computation.16 | convolution fusion | flops 3629187072 | bytes 11808768 | tf_op jit(solution)/shard_map/dot_general | solution.py:57
  362.4 8.6 %convolution_convert_fusion = bf16[3072,768]{1,0:T(8,128)(2,1)} fusion(bf16[768,3072]{1,0:T(8,128)(2,1)} %get-tuple-element.161, f32[768,768]{1,0:T(8,128)S(1)} %copy-done.12), kind=kOutput, calls=%fused_computation.15 | convolution fusion | flops 3626827776 | bytes 11796480 | tf_op jit(solution)/shard_map/dot_general | solution.py:57
  371.1 14.6 %reduce-scatter.10.cloned.1.call-done = bf16[3,768,192]{1,2,0:T(8,128)(2,1)} async-done(((bf16[3,768,768]{1,2,0:T(8,128)(2,1)}), bf16[3,768,192]{1,2,0:T(8,128)(2,1)}) %reduce-scatter.10.cloned.1.call-update) | async-done | bytes 884752 | tf_op jit(solution)/shard_map/reduce_scatter | solution.py:123
  393.2 40.0 %all-reduce.18 = (f32[768]{0:T(1024)S(1)}, f32[768]{0:T(1024)S(1)}, f32[768]{0:T(1024)S(1)}, f32[3072]{0:T(1024)S(1)}, f32[768]{0:T(1024)S(1)}, /*index=5*/f32[768]{0:T(1024)S(1)}, f32[768]{0:T(1024)S(1)}) all-reduce(f32[768]{0:T(1024)S(1)} %get-tuple-element.147, ...), channel_id=9, replica_groups=mesh['dp'=8,'head'=4] {'dp','head'}, use_global_device_ids=true, to_apply=%region_22.23.clone | all-reduce | flops 7680 | bytes 61440
  437.3 11.7 %all-reduce.20 = (f32[12,64]{1,0:T(8,128)S(1)}, f32[12,64]{1,0:T(8,128)S(1)}) all-reduce(f32[12,64]{1,0:T(8,128)S(1)} %copy-done.21, f32[12,64]{1,0:T(8,128)S(1)} %copy-done.31), channel_id=4, replica_groups=mesh['dp'=8,'head'=4] {'head'}, use_global_device_ids=true, to_apply=%region_15.16.clone | all-reduce | flops 1536 | bytes 12288
  449.1 20.3 %all-reduce.19 = (f32[3,64]{1,0:T(4,128)S(1)}, f32[3,64]{1,0:T(4,128)S(1)}) all-reduce(f32[3,64]{1,0:T(4,128)S(1)} %constant_dynamic-slice_fusion.3, f32[3,64]{1,0:T(4,128)S(1)} %constant_dynamic-slice_fusion.1), channel_id=5, replica_groups=mesh['dp'=8,'head'=4] {'dp'}, use_global_device_ids=true, to_apply=%region_16.17.clone | all-reduce | flops 384 | bytes 3072
  477.8 9.9 %reduce-scatter.12.cloned.1.call-done = bf16[24,768]{1,0:T(8,128)(2,1)} async-done(((bf16[768,768]{1,0:T(8,128)(2,1)}), bf16[24,768]{1,0:T(8,128)(2,1)}) %reduce-scatter.12.cloned.1.call-update) | async-done | bytes 36880 | tf_op jit(solution)/shard_map/reduce_scatter | solution.py:123
  489.1 110.7 %reduce-scatter.14.cloned.1.call-done = bf16[24,3072]{1,0:T(8,128)(2,1)} async-done(((bf16[768,3072]{1,0:T(8,128)(2,1)}), bf16[24,3072]{1,0:T(8,128)(2,1)}) %reduce-scatter.14.cloned.1.call-update) | async-done | bytes 147472 | tf_op jit(solution)/shard_map/reduce_scatter | solution.py:123
  601.4 110.3 %reduce-scatter.16.cloned.1.call-done = bf16[96,768]{1,0:T(8,128)(2,1)} async-done(((bf16[3072,768]{1,0:T(8,128)(2,1)}), bf16[96,768]{1,0:T(8,128)(2,1)}) %reduce-scatter.16.cloned.1.call-update) | async-done | bytes 147472 | tf_op jit(solution)/shard_map/reduce_scatter | solution.py:123
  713.3 64.8 %reduce-scatter.18.cloned.1.call-done = bf16[96,576]{1,0:T(8,128)(2,1)} async-done(((bf16[768,576]{1,0:T(8,128)(2,1)}), bf16[96,576]{1,0:T(8,128)(2,1)}) %reduce-scatter.18.cloned.1.call-update) | async-done | bytes 110608
  (231 shorter events, 86.2 us)
Async XLA Ops:
  7.2 44.1 %copy-start = (s32[3,2,8]{2,1,0:T(2,128)S(1)}, s32[3,2,8]{2,1,0:T(2,128)}, u32[]{:S(2)}) copy-start(s32[3,2,8]{2,1,0:T(2,128)} %param.22) | copy-start | bytes 580
  7.2 135.8 %all-gather.9.cloned.1.call-start = ((), (), s32[]{:S(2)}) async-start(), calls=%async_computation.5 | async-start | bytes 4423680 | tf_op jit(solution)/shard_map/all_gather | solution.py:114
  8.3 43.0 %copy-start.35 = (bf16[3,8]{1,0:T(4,128)(2,1)S(1)}, bf16[3,8]{1,0:T(4,128)(2,1)}, u32[]{:S(2)}) copy-start(bf16[3,8]{1,0:T(4,128)(2,1)} %param.24) | copy-start | bytes 148
  8.3 67.0 %copy-start.36 = (bf16[3,8]{1,0:T(4,128)(2,1)S(1)}, bf16[3,8]{1,0:T(4,128)(2,1)}, u32[]{:S(2)}) copy-start(bf16[3,8]{1,0:T(4,128)(2,1)} %param.27) | copy-start | bytes 148
  47.0 49.8 %copy-start.42 = (bf16[24]{0:T(256)(128)(2,1)S(1)}, bf16[24]{0:T(256)(128)(2,1)}, u32[]{:S(2)}) copy-start(bf16[24]{0:T(256)(128)(2,1)} %param.29) | copy-start | bytes 148
  47.0 50.0 %copy-start.43 = (bf16[24]{0:T(256)(128)(2,1)S(1)}, bf16[24]{0:T(256)(128)(2,1)}, u32[]{:S(2)}) copy-start(bf16[24]{0:T(256)(128)(2,1)} %param.30) | copy-start | bytes 148
  47.0 50.2 %copy-start.44 = (bf16[24]{0:T(256)(128)(2,1)S(1)}, bf16[24]{0:T(256)(128)(2,1)}, u32[]{:S(2)}) copy-start(bf16[24]{0:T(256)(128)(2,1)} %param.31) | copy-start | bytes 148
  47.0 50.5 %copy-start.45 = (bf16[24]{0:T(256)(128)(2,1)S(1)}, bf16[24]{0:T(256)(128)(2,1)}, u32[]{:S(2)}) copy-start(bf16[24]{0:T(256)(128)(2,1)} %param.35) | copy-start | bytes 148
  47.0 50.7 %copy-start.46 = (bf16[24]{0:T(256)(128)(2,1)S(1)}, bf16[24]{0:T(256)(128)(2,1)}, u32[]{:S(2)}) copy-start(bf16[24]{0:T(256)(128)(2,1)} %param.36) | copy-start | bytes 148
  47.0 50.9 %copy-start.47 = (bf16[24]{0:T(256)(128)(2,1)S(1)}, bf16[24]{0:T(256)(128)(2,1)}, u32[]{:S(2)}) copy-start(bf16[24]{0:T(256)(128)(2,1)} %param.37) | copy-start | bytes 148
  47.1 51.1 %copy-start.48 = (bf16[96]{0:T(256)(128)(2,1)S(1)}, bf16[96]{0:T(256)(128)(2,1)}, u32[]{:S(2)}) copy-start(bf16[96]{0:T(256)(128)(2,1)} %param.33) | copy-start | bytes 580
  47.1 93.4 %copy-start.3 = (bf16[3,256,768]{2,1,0:T(8,128)(2,1)S(1)}, bf16[3,256,768]{2,1,0:T(8,128)(2,1)}, u32[]{:S(2)}) copy-start(bf16[3,256,768]{2,1,0:T(8,128)(2,1)} %param.20) | copy-start | bytes 3538948
  47.1 95.1 %copy-start.37 = (s32[3,2]{0,1:T(2,128)S(1)}, s32[3,2]{0,1:T(2,128)}, u32[]{:S(2)}) copy-start(s32[3,2]{0,1:T(2,128)} %param.21) | copy-start | bytes 76
  49.1 94.0 %copy-start.39 = (bf16[3,256,768]{2,1,0:T(8,128)(2,1)S(1)}, bf16[3,256,768]{2,1,0:T(8,128)(2,1)}, u32[]{:S(2)}) copy-start(bf16[3,256,768]{2,1,0:T(8,128)(2,1)} %param.19) | copy-start | bytes 3538948
  49.1 130.9 %all-gather.11.cloned.1.call-start = ((), (), s32[]{:S(2)}) async-start(), calls=%async_computation.6 | async-start | bytes 1216512 | tf_op jit(solution)/shard_map/all_gather | solution.py:114
  49.9 151.7 %all-gather.13.cloned.1.call-start = ((), (), s32[]{:S(2)}) async-start(), calls=%async_computation.7 | async-start | bytes 4866048 | tf_op jit(solution)/shard_map/all_gather | solution.py:114
  50.6 215.7 %all-gather.15.cloned.1.call-start = ((), (), s32[]{:S(2)}) async-start(), calls=%async_computation.8 | async-start | bytes 4866048 | tf_op jit(solution)/shard_map/all_gather | solution.py:114
  51.2 334.5 %reduce-scatter.10.cloned.1.call-start = ((), (), s32[]{:S(2)}) async-start(), calls=%async_computation.9 | async-start | bytes 4423680 | tf_op jit(solution)/shard_map/reduce_scatter | solution.py:123
  148.8 15.5 %copy-start.8 = (bf16[3,256,12,64]{1,0,3,2:T(4,128)(2,1)}, bf16[3,256,12,64]{1,0,3,2:T(4,128)(2,1)S(1)}, u32[]{:S(2)}) copy-start(bf16[3,256,12,64]{1,0,3,2:T(4,128)(2,1)S(1)} %reshape.408) | copy-start | bytes 3538948
  183.5 110.7 %copy-start.4 = (f32[768,768]{1,0:T(8,128)}, f32[768,768]{1,0:T(8,128)S(1)}, u32[]{:S(2)}) copy-start(f32[768,768]{1,0:T(8,128)S(1)} %get-tuple-element.160) | copy-start | bytes 7077892
  183.5 18.1 %copy-start.23 = (f32[768]{0:T(1024)S(1)}, f32[768]{0:T(1024)}, u32[]{:S(2)}) copy-start(f32[768]{0:T(1024)} %convert_element_type.210) | copy-start | bytes 9220
  275.9 13.3 %slice-start = ((s8[4718592]{0:T(1024)(128)(4,1)}), s8[4194304]{0:T(1024)(128)(4,1)S(1)}, s32[]{:S(2)}) async-start(s8[4718592]{0:T(1024)(128)(4,1)} %bitcast.180), calls=%async_computation.14 | async-start | bytes 8388608
  278.4 10.7 %copy-start.11 = (f32[768,768]{1,0:T(8,128)}, f32[768,768]{1,0:T(8,128)S(1)}, u32[]{:S(2)}) copy-start(f32[768,768]{1,0:T(8,128)S(1)} %get-tuple-element.146) | copy-start | bytes 7077892
  278.4 10.7 %copy-start.25 = (f32[768]{0:T(1024)S(1)}, f32[768]{0:T(1024)}, u32[]{:S(2)}) copy-start(f32[768]{0:T(1024)} %add_rsqrt_fusion.1) | copy-start | bytes 9220
  318.6 11.2 %copy-start.10 = (bf16[3,256,12,64]{1,0,3,2:T(4,128)(2,1)S(1)}, bf16[3,256,12,64]{1,0,3,2:T(4,128)(2,1)}, u32[]{:S(2)}) copy-start(bf16[3,256,12,64]{1,0,3,2:T(4,128)(2,1)} %reshape.409) | copy-start | bytes 3538948
  347.0 140.7 %reduce-scatter.12.cloned.1.call-start = ((), (), s32[]{:S(2)}) async-start(), calls=%async_computation.10 | async-start | bytes 1216512 | tf_op jit(solution)/shard_map/reduce_scatter | solution.py:123
  351.3 248.5 %reduce-scatter.14.cloned.1.call-start = ((), (), s32[]{:S(2)}) async-start(), calls=%async_computation.11 | async-start | bytes 4866048 | tf_op jit(solution)/shard_map/reduce_scatter | solution.py:123
  360.8 350.9 %reduce-scatter.16.cloned.1.call-start = ((), (), s32[]{:S(2)}) async-start(), calls=%async_computation.12 | async-start | bytes 4866048 | tf_op jit(solution)/shard_map/reduce_scatter | solution.py:123
  371.0 407.1 %reduce-scatter.18.cloned.1.call-start = ((), (), s32[]{:S(2)}) async-start(), calls=%async_computation.13 | async-start | bytes 1105920
  388.3 49.0 %copy-start.21 = (f32[12,64]{1,0:T(8,128)S(1)}, f32[12,64]{1,0:T(8,128)}, u32[]{:S(2)}) copy-start(f32[12,64]{1,0:T(8,128)} %get-tuple-element.168) | copy-start | bytes 9220
  388.3 49.0 %copy-start.31 = (f32[12,64]{1,0:T(8,128)S(1)}, f32[12,64]{1,0:T(8,128)}, u32[]{:S(2)}) copy-start(f32[12,64]{1,0:T(8,128)} %get-tuple-element.170) | copy-start | bytes 9220
  475.4 306.2 %copy-start.1 = (s32[3,2,8]{2,1,0:T(2,128)S(1)}, s32[3,2,8]{2,1,0:T(2,128)}, u32[]{:S(2)}) copy-start(s32[3,2,8]{2,1,0:T(2,128)} %param.22) | copy-start | bytes 580
  (31 other events, 118.5 us)
Sparse Core Ops, SparseCore 0:
  49.2 29.7 all-gather.8
  82.0 54.0 all-gather.10
  139.0 62.5 all-gather.12
  204.3 61.9 all-gather.14
  347.1 38.5 reduce-scatter.9
  390.6 97.0 reduce-scatter.11
  493.2 106.5 reduce-scatter.13
  605.3 106.3 reduce-scatter.15
  715.1 63.0 reduce-scatter.17

commit v2 on v1

--- a/solution.py
+++ b/solution.py
@@ -1,6 +1,10 @@
+import functools
+
 import jax
 import jax.numpy as jnp
 from jax import lax
+from jax.experimental import pallas as pl
+from jax.experimental.pallas import tpu as pltpu
 from jax.sharding import PartitionSpec as P
 
 HD = 64
@@ -107,18 +111,327 @@
     return out.reshape(micro, rows, width), g_in.reshape(micro, rows, width), big, small
 
 
-def body(tokens, cotangent, bucket_ids, seq_lengths, wq, qb, wk, wv, vb, wo, ob, g1, s1, wi, ib, wu, ub, g2, s2):
-    both = ("dp", "head")
+def flipped(j, n_dp, n_head):
+    def one(me, bits):
+        out = me
+        w = 1
+        while w <= bits:
+            if bits & w:
+                out = out + w * (1 - 2 * lax.rem(lax.div(me, w), 2))
+            w *= 2
+        return out
+
+    return one(lax.axis_index("dp"), j // n_head), one(lax.axis_index("head"), j % n_head)
+
+
+def link_orders(n):
+    bits = [1 << b for b in range(n.bit_length() - 2, 0, -1)]
+    if len(bits) == 4:
+        zh, zl, y, x = bits
+        return ((zh, zl, y, x), (zh, zl, x, y), (x, zh, zl, y), (zh, zl, y, x))
+    return (tuple(bits),) * 4
+
+
+def greet(n, n_dp, n_head):
+    barrier = pltpu.get_barrier_semaphore()
+    count = 0
+    b = 1
+    while b < n:
+        pl.semaphore_signal(barrier, inc=1, device_id=flipped(b, n_dp, n_head), device_id_type=pl.DeviceIdType.MESH)
+        count += 1
+        b *= 2
+    pl.semaphore_wait(barrier, count)
+
+
+def subsets(bits):
+    out = [0]
+    for b in bits:
+        out = out + [j | b for j in out]
+    return out
+
+
+def gather_kernel(n_dp, n_head, orders, *refs):
+    parts = len(orders)
+    n = n_dp * n_head
+    src, dst = refs[:parts], refs[parts : 2 * parts]
+    send_sem, recv_sem, own_sem = refs[2 * parts :]
+    place = []
+    for j in range(n):
+        d, h = flipped(j, n_dp, n_head)
+        place.append(d * n_head + h)
+
+    def copy(p, j, b):
+        here = src[p] if j == 0 else dst[p].at[place[j]]
+        k = p * n + (j | b)
+        return pltpu.make_async_remote_copy(
+            src_ref=here,
+            dst_ref=dst[p].at[place[j]],
+            send_sem=send_sem.at[k],
+            recv_sem=recv_sem.at[k],
+            device_id=flipped(b, n_dp, n_head),
+            device_id_type=pl.DeviceIdType.MESH,
+        )
+
+    def arrival(p, j):
+        k = p * n + j
+        return pltpu.make_async_remote_copy(
+            src_ref=src[p],
+            dst_ref=dst[p].at[place[j]],
+            send_sem=send_sem.at[k],
+            recv_sem=recv_sem.at[k],
+            device_id=flipped(1, n_dp, n_head),
+            device_id_type=pl.DeviceIdType.MESH,
+        )
+
+    own = [pltpu.make_async_copy(src[p], dst[p].at[place[0]], own_sem.at[p]) for p in range(parts)]
+    for o in own:
+        o.start()
+    greet(n, n_dp, n_head)
+    started = []
+
+    def start(p, j, b):
+        c = copy(p, j, b)
+        c.start()
+        started.append(c)
+
+    for step in range(len(orders[0]) + 1):
+        for p in range(parts):
+            order = orders[p]
+            fresh = [0] if step == 0 else [j | order[step - 1] for j in subsets(order[: step - 1])]
+            if step == 0:
+                start(p, 0, order[0])
+                start(p, 0, 1)
+                continue
+            old = subsets(order[: step - 1])
+            if step < len(order):
+                for j in old:
+                    start(p, j, order[step])
+            for j in fresh:
+                arrival(p, j).wait_recv()
+                if step < len(order):
+                    start(p, j, order[step])
+                start(p, j, 1)
+    for p in range(parts):
+        for j in subsets(orders[p]):
+            arrival(p, j | 1).wait_recv()
+    for c in started:
+        c.wait_send()
+    for o in own:
+        o.wait()
+
+
+def gather_all(arrays, n_dp, n_head):
+    n = n_dp * n_head
+    parts = len(arrays)
+    any_ = pl.BlockSpec(memory_space=pl.ANY)
+    vmem = pl.BlockSpec(memory_space=pltpu.VMEM)
+    return pl.pallas_call(
+        functools.partial(gather_kernel, n_dp, n_head, link_orders(n)[:parts]),
+        out_shape=[jax.ShapeDtypeStruct((n,) + a.shape, a.dtype) for a in arrays],
+        in_specs=[vmem] * parts,
+        out_specs=[any_] * parts,
+        scratch_shapes=[
+            pltpu.SemaphoreType.DMA((parts * n,)),
+            pltpu.SemaphoreType.DMA((parts * n,)),
+            pltpu.SemaphoreType.DMA((parts,)),
+        ],
+        compiler_params=pltpu.CompilerParams(collective_id=0, has_side_effects=True),
+    )(*arrays)
+
+
+def scatter_kernel(n_dp, n_head, orders, *refs):
+    parts = len(orders)
+    n = n_dp * n_head
+    half = n // 2
+    src, out = refs[:parts], refs[parts : 2 * parts]
+    acc, core, link = (refs[(2 + i) * parts : (3 + i) * parts] for i in range(3))
+    core_send, core_recv, link_send, link_recv, own_sem = refs[5 * parts :]
+    sib = flipped(1, n_dp, n_head)
+    kinds = pl.DeviceIdType.MESH
+
+    def place(j):
+        d, h = flipped(j, n_dp, n_head)
+        return d * n_head + h
+
+    own, core_copy, link_copy = {}, {}, {}
+    for p in range(parts):
+        for j in subsets(orders[p][::-1])[::-1]:
+            k = p * half + j // 2
+            own[p, j] = pltpu.make_async_copy(src[p].at[place(j)], acc[p].at[j // 2], own_sem.at[k])
+            core_copy[p, j] = pltpu.make_async_remote_copy(
+                src_ref=src[p].at[place(j | 1)],
+                dst_ref=core[p].at[j // 2],
+                send_sem=core_send.at[k],
+                recv_sem=core_recv.at[k],
+                device_id=sib,
+                device_id_type=kinds,
+            )
+    for c in own.values():
+        c.start()
+    greet(n, n_dp, n_head)
+
+    def first_of(p):
+        order = orders[p][::-1]
+        return sorted(subsets(order), key=lambda j: [0 if j & b else 1 for b in order])
+
+    for i in range(half):
+        for p in range(parts):
+            core_copy[p, first_of(p)[i]].start()
+
+    def add(into, a, b):
+        rows = a.shape[0]
+        step = 16 if rows % 16 == 0 else rows
+        kind = into.dtype
+
+        def one(i, carry):
+            r = pl.ds(pl.multiple_of(i * step, step), step)
+            into[r, :] = (a[r, :].astype(F32) + b[r, :].astype(F32)).astype(kind)
+            return carry
+
+        lax.fori_loop(0, rows // step, one, 0)
+
+    def send(p, j, b):
+        k = p * half + j // 2
+        c = pltpu.make_async_remote_copy(
+            src_ref=acc[p].at[j // 2],
+            dst_ref=link[p].at[j // 2],
+            send_sem=link_send.at[k],
+            recv_sem=link_recv.at[k],
+            device_id=flipped(b, n_dp, n_head),
+            device_id_type=kinds,
+        )
+        c.start()
+        link_copy[p, j] = c
+
+    steps = len(orders[0])
+
+    def meet(p, j):
+        core_copy[p, j].wait_recv()
+        own[p, j].wait()
+        add(acc[p].at[j // 2], acc[p].at[j // 2], core[p].at[j // 2])
+
+    for p in range(parts):
+        b = orders[p][steps - 1]
+        for j in first_of(p):
+            if j & b:
+                meet(p, j)
+                send(p, j, b)
+    for p in range(parts):
+        b = orders[p][steps - 1]
+        for j in first_of(p):
+            if not j & b:
+                meet(p, j)
+    for t in range(steps - 1, -1, -1):
+        for p in range(parts):
+            b = orders[p][t]
+            left = [j for j in first_of(p) if not any(j & c for c in orders[p][t:])]
+            for j in left:
+                link_copy[p, j | b].wait_recv()
+                into = out[p] if t == 0 else acc[p].at[j // 2]
+                add(into, acc[p].at[j // 2], link[p].at[(j | b) // 2])
+                if t > 0 and j & orders[p][t - 1]:
+                    send(p, j, orders[p][t - 1])
+    for c in core_copy.values():
+        c.wait_send()
+    for c in link_copy.values():
+        c.wait_send()
+
+
+def scatter_all(arrays, n_dp, n_head):
+    n = n_dp * n_head
+    half = n // 2
+    parts = len(arrays)
+    any_ = pl.BlockSpec(memory_space=pl.ANY)
+    vmem = pl.BlockSpec(memory_space=pltpu.VMEM)
+    slots = [pltpu.VMEM((half,) + a.shape[1:], a.dtype) for a in arrays]
+    return pl.pallas_call(
+        functools.partial(scatter_kernel, n_dp, n_head, link_orders(n)[:parts]),
+        out_shape=[jax.ShapeDtypeStruct(a.shape[1:], F32) for a in arrays],
+        in_specs=[any_] * parts,
+        out_specs=[vmem] * parts,
+        scratch_shapes=slots * 3 + [pltpu.SemaphoreType.DMA((parts * half,))] * 5,
+        compiler_params=pltpu.CompilerParams(
+            collective_id=1, has_side_effects=True, vmem_limit_bytes=48 * 1024 * 1024
+        ),
+    )(*arrays)
+
+
+SMALL_ROWS = 8
+
+
+def body(tokens, cotangent, bucket_ids, seq_lengths, *params):
     rows = tokens.shape[1]
     assert rows % LONGEST == 0
+    mask = local_mask(bucket_ids, seq_lengths, rows)
+    n_dp, n_head = lax.axis_size("dp"), lax.axis_size("head")
+    if n_dp * n_head == 32:
+        return kernel_body(tokens, cotangent, mask, n_dp, n_head, *params)
+    return native_body(tokens, cotangent, mask, *params)
+
+
+def kernel_body(tokens, cotangent, mask, n_dp, n_head, wq, qb, wk, wv, vb, wo, ob, g1, s1, wi, ib, wu, ub, g2, s2):
+    n = n_dp * n_head
+    width = wu.shape[1]
+    r, c = wq.shape
+    qkv_rows = 3 * r * c // width
+    lanes = 128
+    small = (qb, vb, ob, g1, s1, ib, ub, g2, s2)
+    sizes = [a.size for a in small]
+    flat = jnp.concatenate([a.reshape(-1).astype(F32) for a in small])
+    pad = SMALL_ROWS * lanes - flat.size
+    flat = jnp.pad(flat, (0, pad)).reshape(SMALL_ROWS, lanes)
+    third = jnp.concatenate([jnp.stack([wq, wk, wv]).reshape(qkv_rows, width), wo], axis=0)
+    gi_, gu_, gt_, gs_ = gather_all([wi.reshape(-1, width), wu, third, flat], n_dp, n_head)
+    wi_ = gi_.reshape(-1, wi.shape[1])
+    wu_ = gu_.reshape(-1, width)
+    wqkv = gt_[:, :qkv_rows].reshape(n_dp, n_head, 3, r, c).transpose(2, 0, 3, 1, 4).reshape(3, n_dp * r, n_head * c)
+    wo_ = gt_[:, qkv_rows:].reshape(-1, width)
+    gs_ = gs_.reshape(n, -1)
+    pieces = []
+    at = 0
+    for a, size in zip(small, sizes):
+        piece = gs_[:, at : at + size]
+        at += size
+        if a.ndim == 2:
+            piece = piece.reshape(n_dp, n_head, *a.shape).transpose(1, 2, 0, 3)
+        pieces.append(piece.reshape(-1))
+    qb_, vb_, ob_, g1_, s1_, ib_, ub_, g2_, s2_ = pieces
+    p = (wqkv[0], qb_, wqkv[1], wqkv[2], vb_, wo_, ob_, g1_, s1_, wi_, ib_, wu_, ub_, g2_, s2_)
+    out, g_in, big, s = layer(tokens, cotangent, mask, p)
+    gqkv = jnp.stack([b.astype(BF16) for b in big[:3]])
+    gqkv = gqkv.reshape(3, n_dp, r, n_head, c).transpose(1, 3, 0, 2, 4).reshape(n, qkv_rows, width)
+    go, gi, gu = (b.astype(BF16) for b in big[3:])
+    third = jnp.concatenate([gqkv, go.reshape(n, -1, width)], axis=1)
+    order = (s[0], s[1], s[2], s[3], s[4], s[5], s[6], s[7], s[8])
+    flat = []
+    for a, g in zip(small, order):
+        if a.ndim == 2:
+            h, k = a.shape
+            g = g.reshape(n_head, h, n_dp, k).transpose(2, 0, 1, 3)
+        flat.append(g.reshape(n, -1))
+    flat = jnp.pad(jnp.concatenate(flat, axis=1), ((0, 0), (0, pad))).reshape(n, SMALL_ROWS, lanes)
+    gi, gu, third, flat = scatter_all(
+        [gi.reshape(n, -1, width), gu.reshape(n, -1, width), third, flat], n_dp, n_head
+    )
+    gqkv = third[:qkv_rows].reshape(3, r, c)
+    flat = flat.reshape(-1)
+    pieces = []
+    at = 0
+    for a, size in zip(small, sizes):
+        pieces.append(flat[at : at + size].reshape(a.shape))
+        at += size
+    gqb, gvb, gob, gg1, gs1, gib, gub, gg2, gs2 = pieces
+    return (out, g_in, gqkv[0], gqb, gqkv[1], gqkv[2], gvb, third[qkv_rows:], gob, gg1, gs1, gi.reshape(wi.shape), gib, gu, gub, gg2, gs2)
+
+
+def native_body(tokens, cotangent, mask, wq, qb, wk, wv, vb, wo, ob, g1, s1, wi, ib, wu, ub, g2, s2):
+    both = ("dp", "head")
     ag = lambda a, ax, dim: lax.all_gather(a, ax, axis=dim, tiled=True)
-    n_head = lax.axis_size("head")
     wqkv = ag(jnp.stack([wq, wk, wv]), "dp", 1)
     wqkv = ag(wqkv, "head", 2)
     ob_, g1_, s1_, ub_, g2_, s2_, ib_ = (ag(a, both, 0) for a in (ob, g1, s1, ub, g2, s2, ib))
     qb_, vb_ = (ag(ag(a, "dp", 1), "head", 0) for a in (qb, vb))
     p = (wqkv[0], qb_, wqkv[1], wqkv[2], vb_, ag(wo, both, 0), ob_, g1_, s1_, ag(wi, both, 0), ib_, ag(wu, both, 0), ub_, g2_, s2_)
-    mask = local_mask(bucket_ids, seq_lengths, rows)
     out, g_in, big, small = layer(tokens, cotangent, mask, p)
     sc = lambda a, ax, dim: lax.psum_scatter(a, ax, scatter_dimension=dim, tiled=True)
     gqkv = jnp.stack([b.astype(BF16) for b in big[:3]])

time: 793 us -> 475 us (0.60)
  waiting for transfers between devices: 383 us -> 0 us
  Pallas kernels: 0 us -> 198 us
  blocking collectives: 195 us -> 0 us
  local copies, waits for them, and re-layouts: 47.9 us -> 124 us
  between operations: 16.2 us -> 2.09 us
    reduce_scatter x4 -> x0, waiting for transfers between devices: 245 us -> none  [body(): lax.psum_scatter(a, ax, scatter_dimension=dim, tiled=True)]
    pallas_call x0 -> x2, Pallas kernels: none -> 198 us  [the longest x1 109 us: scatter_all(): pl.pallas_call(functools.partial(scatter_kernel, n_dp, n_head, link_order...]
    unnamed x4 -> x0, blocking collectives: 111 us -> none
    all_gather x5 -> x0, blocking collectives: 83.9 us -> none  [body(): ag = lambda a, ax, dim: lax.all_gather(a, ax, axis=dim, tiled=True)]
    all_gather x4 -> x0, waiting for transfers between devices: 70.7 us -> none  [body(): ag = lambda a, ax, dim: lax.all_gather(a, ax, axis=dim, tiled=True)]
    unnamed x10 -> x0, waiting for transfers between devices: 66.8 us -> none
    reshape x0 -> x21, local copies, waits for them, and re-layouts: none -> 42.4 us  [the longest x2 12.9 us: kernel_body(): gt_[:, :qkv_rows].reshape(n_dp, n_head, 3, r, c).transpose(2, 0, 3, 1, 4)]
    another operation x1 -> x6, local copies, waits for them, and re-layouts: 0.13 us -> 17.6 us  [kernel_body(): gqkv = jnp.stack([b.astype(BF16) for b in big[:3]])]
  transfers between devices with their start and end apart: 9 -> 0, of which waited for: 7 -> 0; matrix products, arithmetic and copies ran while one was open for 13% -> 0% of each run, Pallas kernels for 0% -> 0%
where the time goes in v2:
time: 475 us; the launch traced here: 470 us
  Pallas kernels  198 us (42%)
  local copies, waits for them, and re-layouts  124 us (26%)
  matrix products  114 us (24%)
  other arithmetic  31.9 us (7%)
    pallas_call x1, Pallas kernels, scatter_all(): pl.pallas_call(functools.partial(scatter_kernel, n_dp, n_head, link_order...  109 us
    pallas_call x1, Pallas kernels, gather_all(): pl.pallas_call(functools.partial(gather_kernel, n_dp, n_head, link_orders...  88.9 us
    dot_general x6, matrix products, mm(): return jnp.dot(a, b, preferred_element_type=F32)  33.5 us
    dot_general x6, matrix products, mm_nt(): lax.dot_general(a, b, (((1,), (1,)), ((), ())), preferred_element_type=F32)  23.4 us
    dot_general x6, matrix products, mm_tn(): lax.dot_general(a, b, (((0,), (0,)), ((), ())), preferred_element_type=F32)  22.8 us
    another operation x6, local copies, waits for them, and re-layouts, kernel_body(): gqkv = jnp.stack([b.astype(BF16) for b in big[:3]])  17.6 us
    reshape x2, local copies, waits for them, and re-layouts, kernel_body(): gt_[:, :qkv_rows].reshape(n_dp, n_head, 3, r, c).transpose(2, 0, 3, 1, 4)  12.9 us
    convert_element_type x1, other arithmetic, layer(): ds = (probs * (dprobs - inner)).astype(BF16)  11.2 us

profile of v2, /device:TPU:0, one launch (start us, length us, event | category | flops | bytes accessed | tf_op | source)
XLA Modules:
  0.0 470.3 jit_solution(1177437383708889615)
XLA Ops:
  8.6 4.8 %concatenate.15 = bf16[288]{0:T(512)(128)(2,1)S(1)} concatenate(bf16[24]{0:T(256)(128)(2,1)S(1)} %convert_element_type.151, bf16[24]{0:T(256)(128)(2,1)S(1)} %convert_element_type.152, bf16[24]{0:T(256)(128)(2,1)} %param.29, bf16[24]{0:T(256)(128)(2,1)} %param.30, bf16[24]{0:T(256)(128)(2,1)} %param.31, bf16[96]{0:T(256)(128)(2,1)} %param.33, bf16[24]{0:T(256)(128)(2,1)} %param.35, ...), dimensions={0} | concatenate | bytes 1152 | tf_op jit(solution)/shard_map/concatenate | solution.py:380
  14.0 88.9 %shard_map.314 = (bf16[32,96,768]{2,1,0:T(8,128)(2,1)}, bf16[32,96,768]{2,1,0:T(8,128)(2,1)}, bf16[32,96,768]{2,1,0:T(8,128)(2,1)}, f32[32,8,128]{2,1,0:T(8,128)}) custom-call(bf16[96,768]{1,0:T(8,128)(2,1)} %reshape.491.refs_0_, bf16[96,768]{1,0:T(8,128)(2,1)} %refs_1_.1, bf16[96,768]{1,0:T(8,128)(2,1)} %pad_maximum_fusion.2.refs_2_, ...), custom_call_target="tpu_custom_call" | custom-call | tf_op jit(solution)/shard_map/pallas_call | solution.py:228
  107.6 5.9 %reshape.495 = bf16[8,4,3,96,192]{4,3,2,1,0:T(8,128)(2,1)} reshape(bf16[32,72,768]{2,1,0:T(8,128)(2,1)S(1)} %slice.95) | data formatting | bytes 7077888 | tf_op jit(solution)/shard_map/reshape | solution.py:387
  113.5 7.0 %copy.76 = bf16[8,4,3,96,192]{3,0,4,1,2:T(8,128)(2,1)} copy(bf16[8,4,3,96,192]{4,3,2,1,0:T(8,128)(2,1)} %reshape.495) | data formatting | bytes 7077888 | tf_op jit(solution)/shard_map/reshape | solution.py:387
  120.6 3.8 fusion.78
  126.5 3.8 fusion.29
  132.6 4.2 squeeze.22
  136.9 3.8 fusion.36
  140.6 3.8 reshape.501
  144.4 8.3 %fusion.83 = (f32[3,12,256]{2,1,0:T(8,128)S(1)}, f32[3,12,256,256]{2,3,1,0:T(8,128)}) fusion(pred[3,256,256]{1,2,0:T(8,128)(4,1)S(1)} %copy-done.30, bf16[3,256,12,64]{1,0,3,2:T(4,128)(2,1)} %reshape.501, bf16[3,256,12,64]{1,0,3,2:T(4,128)(2,1)S(1)} %reshape.500), kind=kOutput, calls=%fused_computation.139 | convolution fusion | flops 311427328 | bytes 12029952 | tf_op jit(solution)/shard_map/sub | solution.py:79
  154.2 3.8 fusion.28
  160.7 5.1 %fusion.33 = bf16[3,256,12,64]{1,3,2,0:T(8,128)(2,1)S(1)} fusion(bf16[3,256,12,64]{1,0,3,2:T(4,128)(2,1)S(1)} %reshape.498, f32[3,12,256,256]{2,3,1,0:T(8,128)} %get-tuple-element.74, f32[3,12,256]{2,1,0:T(8,128)S(1)} %get-tuple-element.73), kind=kOutput, calls=%fused_computation.72 | convolution fusion | flops 307298304 | bytes 11833344 | tf_op jit(solution)/shard_map/mhqk,mkhd->mqhd/dot_general | solution.py:81
  173.8 8.5 %reshape.504 = bf16[768,3072]{1,0:T(8,128)(2,1)} reshape(bf16[32,96,768]{2,1,0:T(8,128)(2,1)} %get-tuple-element.27) | data formatting | bytes 9437184 | tf_op jit(solution)/shard_map/reshape | solution.py:385
  182.3 10.7 %multiply_convert_fusion.1 = (bf16[768,3072]{1,0:T(8,128)(2,1)}, f32[768,3072]{1,0:T(8,128)}) fusion(f32[3072]{0:T(1024)S(1)} %add.186, bf16[768,3072]{1,0:T(8,128)(2,1)} %reshape.504, f32[768,768]{1,0:T(8,128)S(1)} %get-tuple-element.76, f32[768]{0:T(1024)S(1)} %add.183, f32[768]{0:T(1024)S(1)} %mul.184, f32[768]{0:T(1024)S(1)} %add_rsqrt_fusion.1, ...), kind=kOutput, calls=%fused_computation.10 | convolution fusion | flops 3640983552 | bytes 21258240 | tf_op jit(solution)/shard_map/dot_general | solution.py:53
  193.1 8.5 %fusion.93 = (f32[768]{0:T(1024)S(1)}, f32[768,768]{1,0:T(8,128)S(1)}) fusion(f32[768]{0:T(1024)S(1)} %add.192, bf16[768,3072]{1,0:T(8,128)(2,1)} %get-tuple-element.77, bf16[3072,768]{1,0:T(8,128)(2,1)} %bitcast.194, f32[768]{0:T(1024)S(1)} %add.183, f32[768]{0:T(1024)S(1)} %mul.184, f32[768]{0:T(1024)S(1)} %add_rsqrt_fusion.1, f32[768,768]{1,0:T(8,128)} %copy-done.5, ...), kind=kOutput, calls=%fused_computation.141 | convolution fusion | flops 3628006656 | bytes 14174208 | tf_op jit(solution)/shard_map/dot_general | solution.py:53
  209.4 3.4 convert_reduce_fusion.2
  212.9 10.3 %convert_reduce_fusion = (f32[3072]{0:T(1024)S(1)}, bf16[768,3072]{1,0:T(8,128)(2,1)S(1)}) fusion(f32[768,3072]{1,0:T(8,128)} %get-tuple-element.78, f32[3072]{0:T(1024)S(1)} %copy-done.46, bf16[3072,768]{1,0:T(8,128)(2,1)} %bitcast.195, f32[768,768]{1,0:T(8,128)S(1)} %get-tuple-element.42), kind=kOutput, calls=%fused_computation.7 | convolution fusion | flops 3655136256 | bytes 21258240 | tf_op jit(solution)/shard_map/dot_general | solution.py:57
  223.3 4.5 multiply_reduce_fusion.1
  232.4 3.4 reshape.533
  238.7 5.8 %convert_reduce_fusion.4 = (f32[12,64]{1,0:T(8,128)S(1)}, bf16[3,256,12,64]{1,3,2,0:T(8,128)(2,1)S(1)}) fusion(bf16[3,256,12,64]{1,3,2,0:T(8,128)(2,1)} %copy.85, f32[3,12,256,256]{2,3,1,0:T(8,128)} %get-tuple-element.74, f32[3,12,256]{2,1,0:T(8,128)S(1)} %copy-done.37), kind=kOutput, calls=%fused_computation.37 | convolution fusion | flops 308477184 | bytes 11836416 | tf_op jit(solution)/shard_map/mhqk,mqhd->mkhd/dot_general | solution.py:105
  244.7 7.3 %multiply_reduce_fusion = (f32[3,12,256]{2,1,0:T(8,128)S(1)}, f32[3,12,256,256]{2,3,1,0:T(8,128)}) fusion(f32[3,12,256,256]{2,3,1,0:T(8,128)} %get-tuple-element.74, f32[3,12,256]{2,1,0:T(8,128)S(1)} %copy-done.37, bf16[3,256,12,64]{1,3,2,0:T(8,128)(2,1)} %copy.85, bf16[3,256,12,64]{1,0,3,2:T(4,128)(2,1)S(1)} %copy-done.21), kind=kOutput, calls=%fused_computation.9 | convolution fusion | flops 309058560 | bytes 21307392 | tf_op jit(solution)/shard_map/mqhd,mkhd->mhqk/dot_general | solution.py:99
  251.9 11.2 %multiply_convert_fusion = bf16[3,12,256,256]{2,3,1,0:T(8,128)(2,1)} fusion(f32[3,12,256,256]{2,3,1,0:T(8,128)} %get-tuple-element.83, f32[3,12,256]{2,1,0:T(8,128)S(1)} %get-tuple-element.82, f32[3,12,256,256]{2,3,1,0:T(8,128)} %get-tuple-element.74, f32[3,12,256]{2,1,0:T(8,128)S(1)} %copy-done.37), kind=kLoop, calls=%fused_computation.8 | loop fusion | flops 9437184 | bytes 23666688 | tf_op jit(solution)/shard_map/convert_element_type | solution.py:101
  263.2 4.3 convert_reduce_fusion.5
  280.9 4.1 stack.28
  288.1 3.9 fusion.41
  296.5 4.1 stack.29
  303.7 3.7 maximum_bitcast_fusion
  307.5 8.8 %reshape.514 = bf16[32,72,768]{2,1,0:T(8,128)(2,1)} reshape(bf16[8,4,3,96,192]{4,3,2,1,0:T(8,128)(2,1)} %maximum_bitcast_fusion) | data formatting | bytes 7077888 | tf_op jit(solution)/shard_map/reshape | solution.py:402
  321.6 8.5 %convolution_convert_fusion = bf16[3072,768]{1,0:T(8,128)(2,1)} fusion(bf16[768,3072]{1,0:T(8,128)(2,1)} %get-tuple-element.77, f32[768,768]{1,0:T(8,128)S(1)} %copy-done.19), kind=kOutput, calls=%fused_computation.15 | convolution fusion | flops 3626827776 | bytes 11796480 | tf_op jit(solution)/shard_map/dot_general | solution.py:61
  330.1 6.5 %convolution_convert_fusion.1 = bf16[768,3072]{1,0:T(8,128)(2,1)} fusion(bf16[768,3072]{1,0:T(8,128)(2,1)S(1)} %bitcast.204, f32[768,768]{1,0:T(8,128)S(1)} %copy-done.7, f32[768]{0:T(1024)S(1)} %copy-done.48, f32[768]{0:T(1024)S(1)} %copy-done.39, f32[768]{0:T(1024)S(1)} %copy-done.43, f32[768]{0:T(1024)S(1)} %broadcast_multiply_fusion.5), kind=kOutput, calls=%fused_computation.16 | convolution fusion | flops 3629187072 | bytes 11808768 | tf_op jit(solution)/shard_map/dot_general | solution.py:61
  336.6 8.5 %reshape.512.refs_0_ = bf16[32,96,768]{2,1,0:T(8,128)(2,1)} reshape(bf16[768,3072]{1,0:T(8,128)(2,1)} %convolution_convert_fusion.1) | data formatting | bytes 9437184 | tf_op jit(solution)/shard_map/reshape | solution.py:414
  347.4 109.2 %shard_map.315 = (f32[96,768]{1,0:T(8,128)S(1)}, f32[96,768]{1,0:T(8,128)S(1)}, f32[96,768]{1,0:T(8,128)S(1)}, f32[8,128]{1,0:T(8,128)S(1)}) custom-call(bf16[32,96,768]{2,1,0:T(8,128)(2,1)S(1)} %copy-done.2, bf16[32,96,768]{2,1,0:T(8,128)(2,1)} %bitcast.166, bf16[32,96,768]{2,1,0:T(8,128)(2,1)} %pad_maximum_fusion.refs_2_, f32[32,8,128]{2,1,0:T(8,128)S(1)} %bitcast.158), custom_call_target="tpu_custom_call" | custom-call | tf_op jit(solution)/shard_map/pallas_call | solution.py:347
  (217 shorter events, 89.9 us)
Async XLA Ops:
  132.6 11.8 %copy-start.10 = (bf16[3,256,12,64]{1,0,3,2:T(4,128)(2,1)}, bf16[3,256,12,64]{1,0,3,2:T(4,128)(2,1)S(1)}, u32[]{:S(2)}) copy-start(bf16[3,256,12,64]{1,0,3,2:T(4,128)(2,1)S(1)} %reshape.500) | copy-start | bytes 3538948
  144.4 8.3 %copy-start.31 = (f32[32,24]{1,0:T(8,128)S(1)}, f32[32,24]{1,0:T(8,128)}, u32[]{:S(2)}) copy-start(f32[32,24]{1,0:T(8,128)} %get-tuple-element.62) | copy-start | bytes 9220
  152.7 8.0 %copy-start.36 = (f32[3,12,256]{2,1,0:T(8,128)}, f32[3,12,256]{2,1,0:T(8,128)S(1)}, u32[]{:S(2)}) copy-start(f32[3,12,256]{2,1,0:T(8,128)S(1)} %get-tuple-element.73) | copy-start | bytes 110596
  154.2 3.9 copy-start.14
  160.7 5.1 %copy-start.20 = (bf16[3,256,12,64]{1,0,3,2:T(4,128)(2,1)}, bf16[3,256,12,64]{1,0,3,2:T(4,128)(2,1)S(1)}, u32[]{:S(2)}) copy-start(bf16[3,256,12,64]{1,0,3,2:T(4,128)(2,1)S(1)} %reshape.498) | copy-start | bytes 3538948
  167.1 4.8 %copy-start.25 = (bf16[96,8,3,256]{3,1,2,0:T(8,128)(2,1)}, bf16[96,8,3,256]{3,1,2,0:T(8,128)(2,1)S(1)}, u32[]{:S(2)}) copy-start(bf16[96,8,3,256]{3,1,2,0:T(8,128)(2,1)S(1)} %copy.109) | copy-start | bytes 3538948
  172.0 10.3 %copy-start.5 = (f32[768,768]{1,0:T(8,128)}, f32[768,768]{1,0:T(8,128)S(1)}, u32[]{:S(2)}) copy-start(f32[768,768]{1,0:T(8,128)S(1)} %get-tuple-element.76) | copy-start | bytes 7077892
  172.5 20.7 %copy-start.42 = (f32[768]{0:T(1024)}, f32[768]{0:T(1024)S(1)}, u32[]{:S(2)}) copy-start(f32[768]{0:T(1024)S(1)} %add_rsqrt_fusion.1) | copy-start | bytes 9220
  172.8 20.3 %copy-start.38 = (f32[768]{0:T(1024)}, f32[768]{0:T(1024)S(1)}, u32[]{:S(2)}) copy-start(f32[768]{0:T(1024)S(1)} %mul.184) | copy-start | bytes 9220
  172.9 20.2 %copy-start.47 = (f32[768]{0:T(1024)}, f32[768]{0:T(1024)S(1)}, u32[]{:S(2)}) copy-start(f32[768]{0:T(1024)S(1)} %add.183) | copy-start | bytes 9220
  173.8 8.5 %copy-start.45 = (f32[3072]{0:T(1024)}, f32[3072]{0:T(1024)S(1)}, u32[]{:S(2)}) copy-start(f32[3072]{0:T(1024)S(1)} %add.186) | copy-start | bytes 36868
  182.3 10.7 %copy-start.32 = (f32[32,24]{1,0:T(8,128)S(1)}, f32[32,24]{1,0:T(8,128)}, u32[]{:S(2)}) copy-start(f32[32,24]{1,0:T(8,128)} %get-tuple-element.57) | copy-start | bytes 9220
  209.4 13.8 %slice-start = ((s8[4718592]{0:T(1024)(128)(4,1)}), s8[4194304]{0:T(1024)(128)(4,1)S(1)}, s32[]{:S(2)}) async-start(s8[4718592]{0:T(1024)(128)(4,1)} %bitcast.167), calls=%async_computation | async-start | bytes 8388608
  212.8 10.4 %copy-start.18 = (f32[768,768]{1,0:T(8,128)}, f32[768,768]{1,0:T(8,128)S(1)}, u32[]{:S(2)}) copy-start(f32[768,768]{1,0:T(8,128)S(1)} %get-tuple-element.42) | copy-start | bytes 7077892
  212.8 10.4 %copy-start.6 = (f32[768,768]{1,0:T(8,128)S(1)}, f32[768,768]{1,0:T(8,128)}, u32[]{:S(2)}) copy-start(f32[768,768]{1,0:T(8,128)} %copy-done.5) | copy-start | bytes 7077892
  212.8 10.4 %slice-start.1 = ((s8[4718592]{0:T(1024)(128)(4,1)}), s8[524288]{0:T(1024)(128)(4,1)S(1)}, s32[]{:S(2)}) async-start(s8[4718592]{0:T(1024)(128)(4,1)} %bitcast.167), calls=%async_computation.1 | async-start | bytes 1048576
  212.8 10.4 %copy-start.39 = (f32[768]{0:T(1024)S(1)}, f32[768]{0:T(1024)}, u32[]{:S(2)}) copy-start(f32[768]{0:T(1024)} %copy-done.38) | copy-start | bytes 9220
  212.9 10.4 %copy-start.43 = (f32[768]{0:T(1024)S(1)}, f32[768]{0:T(1024)}, u32[]{:S(2)}) copy-start(f32[768]{0:T(1024)} %copy-done.42) | copy-start | bytes 9220
  223.2 4.6 copy-start.52
  238.7 6.0 %copy-start.21 = (bf16[3,256,12,64]{1,0,3,2:T(4,128)(2,1)S(1)}, bf16[3,256,12,64]{1,0,3,2:T(4,128)(2,1)}, u32[]{:S(2)}) copy-start(bf16[3,256,12,64]{1,0,3,2:T(4,128)(2,1)} %copy-done.20) | copy-start | bytes 3538948
  251.9 11.2 %copy-start.13 = (bf16[3,256,12,64]{1,0,3,2:T(4,128)(2,1)S(1)}, bf16[3,256,12,64]{1,0,3,2:T(4,128)(2,1)}, u32[]{:S(2)}) copy-start(bf16[3,256,12,64]{1,0,3,2:T(4,128)(2,1)} %reshape.501) | copy-start | bytes 3538948
  263.2 4.9 %copy-start.41 = (f32[768]{0:T(1024)S(1)}, f32[768]{0:T(1024)}, u32[]{:S(2)}) copy-start(f32[768]{0:T(1024)} %get-tuple-element.41) | copy-start | bytes 9220
  263.2 4.9 %copy-start.44 = (f32[768]{0:T(1024)S(1)}, f32[768]{0:T(1024)}, u32[]{:S(2)}) copy-start(f32[768]{0:T(1024)} %get-tuple-element.35) | copy-start | bytes 9220
  263.2 5.0 %copy-start.40 = (f32[768]{0:T(1024)S(1)}, f32[768]{0:T(1024)}, u32[]{:S(2)}) copy-start(f32[768]{0:T(1024)} %get-tuple-element.39) | copy-start | bytes 9220
  275.1 3.8 copy-start.50
  280.9 7.2 %copy-start.11 = (bf16[3,256,12,64]{1,0,3,2:T(4,128)(2,1)S(1)}, bf16[3,256,12,64]{1,0,3,2:T(4,128)(2,1)}, u32[]{:S(2)}) copy-start(bf16[3,256,12,64]{1,0,3,2:T(4,128)(2,1)} %copy-done.10) | copy-start | bytes 3538948
  296.5 7.3 %copy-start.12 = (bf16[1,8,96,4,192]{4,2,0,3,1:T(8,128)(2,1)S(1)}, bf16[1,8,96,4,192]{4,2,0,3,1:T(8,128)(2,1)}, u32[]{:S(2)}) copy-start(bf16[1,8,96,4,192]{4,2,0,3,1:T(8,128)(2,1)} %copy.96) | copy-start | bytes 3538948
  307.5 8.8 %copy-start.9 = (f32[768,768]{1,0:T(8,128)S(1)}, f32[768,768]{1,0:T(8,128)}, u32[]{:S(2)}) copy-start(f32[768,768]{1,0:T(8,128)} %copy-done.8) | copy-start | bytes 7077892
  318.8 11.2 %slice-start.2 = ((s8[4718592]{0:T(1024)(128)(4,1)}), s8[524288]{0:T(1024)(128)(4,1)S(1)}, s32[]{:S(2)}) async-start(s8[4718592]{0:T(1024)(128)(4,1)} %bitcast.203), calls=%async_computation.2 | async-start | bytes 1048576
  321.6 8.5 %copy-start.7 = (f32[768,768]{1,0:T(8,128)S(1)}, f32[768,768]{1,0:T(8,128)}, u32[]{:S(2)}) copy-start(f32[768,768]{1,0:T(8,128)} %copy-done.5) | copy-start | bytes 7077892
  321.6 8.5 %copy-start.48 = (f32[768]{0:T(1024)S(1)}, f32[768]{0:T(1024)}, u32[]{:S(2)}) copy-start(f32[768]{0:T(1024)} %copy-done.47) | copy-start | bytes 9220
  321.6 8.5 %slice-start.3 = ((s8[4718592]{0:T(1024)(128)(4,1)}), s8[4194304]{0:T(1024)(128)(4,1)S(1)}, s32[]{:S(2)}) async-start(s8[4718592]{0:T(1024)(128)(4,1)} %bitcast.203), calls=%async_computation.3 | async-start | bytes 8388608
  (25 other events, 50.1 us)
